TPU v7x, 128 devices: a whole 4x4x4 slice. The times are simulated.
128 devices in a mesh: el: 8 (over y, x_lo), ph: 16 (over x_hi, z, core).
Axes of the slice: x: 4 (x_hi: 2, x_lo: 2; x = x_hi * 2 + x_lo), y: 4, z: 4, core: 2. Of those that a mesh axis runs over, the one named last changes fastest.
Arguments:
- elec_dev: float32 [128, 96, 256], P(('el', 'ph')), may hold values from -6 to 6
- phon_dev: float32 [16, 24, 96, 256], P('ph', 'el'), may hold values from -6 to 6
- elec_source: float32 [128, 96, 256], P(('el', 'ph')), may hold values from -6 to 6
- phon_source: float32 [16, 24, 96, 256], P('ph', 'el'), may hold values from -6 to 6
- elec_rate: float32 [128, 256], P(('el', 'ph')), may hold values from 0.75 to 3
- phon_rate: float32 [16, 24, 256], P('ph', 'el'), may hold values from 0.75 to 3
- tiles: bfloat16 [8, 16, 128, 256, 256], P('el', 'ph'), may hold values from -0.046875 to 0.046875
- tile_rows: int32 [8, 16, 128], P('el', 'ph'), may hold values from 0 to 15, as said below
- tile_cols: int32 [8, 16, 128], P('el', 'ph'), may hold values from 0 to 23, as said below
- tile_count: int32 [8, 16], P('el', 'ph'), may hold values from 16 to 128, as said below
Outputs:
- elec_out: float32 [128, 96, 256], P(('el', 'ph'))
- phon_out: float32 [16, 24, 96, 256], P('ph', 'el')
Inputs may be any that keep to these rules, and one draw needn't show every extreme that they name: `tile_rows`: block of each slot's tile among the 16 electron blocks of its pattern row; the slots of one cell name distinct (row, column) pairs. `tile_cols`: block of each slot's tile among the 24 phonon blocks of its pattern column. Slots 0 to tile_count - 1 of a cell are live; some cell is full in every draw.
All inputs are finite; a program needn't handle non-finite values.
Results may differ from a plain program's by a relative error of at most 0.0021.
Values may be sent and summed in bfloat16 or wider, within the bound.
A program may use at most 128 MiB of HBM per device.

v0:
```python
import jax
import jax.numpy as jnp
from jax import lax
from jax.sharding import Mesh
from jax.sharding import PartitionSpec as P

ITERS = 3
EL = ("el_0", "el_1")
EL_PH = ("el_0", "el_1", "ph")


tile_group = 8


def copy_for_each(shard, axis):
    copies = jnp.broadcast_to(shard, (lax.axis_size(axis), *shard.shape))
    return lax.all_to_all(copies, axis, split_axis=0, concat_axis=0, tiled=True)


def joined_along(tiles, dim):
    tiles = jnp.moveaxis(tiles, 0, dim)
    dims = tiles.shape
    return tiles.reshape(*dims[:dim], dims[dim] * dims[dim + 1], *dims[dim + 2 :])


def gather_directly(shard, axis, dim):
    tiles = copy_for_each(shard, axis)
    return joined_along(tiles, dim)


def split_up(shard, dim, size):
    before, after = (shard.shape[:dim], shard.shape[dim + 1 :])
    return jnp.moveaxis(shard.reshape(*before, size, -1, *after), dim, 0)


def summed_on_arrival(shard, axis, dim):
    tiles = split_up(shard, dim, lax.axis_size(axis))
    arrived = lax.all_to_all(tiles, axis, split_axis=0, concat_axis=0, tiled=True)
    return arrived.sum(axis=0)


def gather_axes(shard, axes, dim):
    if not axes:
        return shard
    nearer = lax.all_gather(shard, axes[-1], axis=dim, tiled=True)
    return gather_axes(nearer, axes[:-1], dim)


def tile_pass(tile_set, row_ids, col_ids, first_slot, end_slot, elec_blocks, phon_blocks):
    zero_totals = (
        jnp.zeros(elec_blocks.shape, jnp.float32),
        jnp.zeros(phon_blocks.shape, jnp.float32),
    )

    def one_group(group_index, totals):
        elec_total, phon_total = totals
        slot_start = group_index * tile_group
        block_tiles = lax.dynamic_slice_in_dim(tile_set, slot_start, tile_group, 0)
        group_rows = lax.dynamic_slice_in_dim(row_ids, slot_start, tile_group, 0)
        group_cols = lax.dynamic_slice_in_dim(col_ids, slot_start, tile_group, 0)
        places = slot_start + jnp.arange(tile_group, dtype=jnp.int32)
        active = (places >= first_slot) & (places < end_slot)
        weight_mask = jnp.where(active, 1.0, 0.0).astype(jnp.float32)[:, None, None]
        elec_in = jnp.take(elec_blocks, group_rows, axis=0)
        phon_in = jnp.take(phon_blocks, group_cols, axis=0)
        to_phonon = (
            jnp.einsum("tka,tab->tkb", elec_in, block_tiles, preferred_element_type=jnp.float32)
            * weight_mask
        )
        to_electron = (
            jnp.einsum("tkb,tab->tka", phon_in, block_tiles, preferred_element_type=jnp.float32)
            * weight_mask
        )
        elec_total = elec_total.at[group_rows].add(to_electron)
        phon_total = phon_total.at[group_cols].add(to_phonon)
        return (elec_total, phon_total)

    return lax.fori_loop(
        first_slot // tile_group, (end_slot + tile_group - 1) // tile_group, one_group, zero_totals
    )


def local(
    elec_dev,
    phon_dev,
    elec_source,
    phon_source,
    elec_rate,
    phon_rate,
    tiles,
    tile_rows,
    tile_cols,
    tile_count,
):
    tile_set = tiles[0, 0]
    row_ids = tile_rows[0, 0]
    col_ids = tile_cols[0, 0]
    live_count = tile_count[0]
    own_end = live_count[0]
    elec_range = gather_directly(elec_dev.astype(jnp.bfloat16), "ph", 0)
    phon_range = gather_directly(phon_dev[0].astype(jnp.bfloat16), EL, 0)
    elec_now = elec_dev
    phon_now = phon_dev[0]
    for sweep_index in range(ITERS):
        elec_drag, phon_drag = tile_pass(
            tile_set, row_ids, col_ids, 0, own_end, elec_range, phon_range
        )
        elec_now = (elec_source + summed_on_arrival(elec_drag, "ph", 0)) / elec_rate[:, None, :]
        phon_now = (phon_source[0] + summed_on_arrival(phon_drag, EL, 0)) / phon_rate[0][:, None, :]
        if sweep_index + 1 < ITERS:
            elec_range = gather_directly(elec_now.astype(jnp.bfloat16), "ph", 0)
            phon_range = gather_axes(phon_now.astype(jnp.bfloat16), EL, 0)
    return (elec_now, phon_now[None])


def solution(mesh):
    split = Mesh(mesh.devices.reshape(4, 2, mesh.shape["ph"]), ("el_0", "el_1", "ph"))
    placed = (
        P(EL_PH, None, None),
        P("ph", EL, None, None),
        P(EL_PH, None, None),
        P("ph", EL, None, None),
        P(EL_PH, None),
        P("ph", EL, None),
        P(EL, "ph", None, None, None),
        P(EL, "ph", None),
        P(EL, "ph", None),
        P(EL, "ph"),
    )
    return jax.shard_map(
        local,
        mesh=split,
        in_specs=placed,
        out_specs=(P(EL_PH, None, None), P("ph", EL, None, None)),
        check_vma=False,
    )
```

profile of v0, /device:TPU:0, one launch (start us, length us, event | category | flops | bytes accessed | tf_op | source)
XLA Modules:
  0.0 854.8 jit_solution(704319720557261080)
XLA Ops:
  9.1 8.0 all-to-all-start.1
  17.2 15.2 %all-to-all-done.1 = bf16[16,1,96,256]{3,2,1,0:T(8,128)(2,1)} async-done(((bf16[16,1,96,256]{3,2,1,0:T(8,128)(2,1)}), bf16[16,1,96,256]{3,2,1,0:T(8,128)(2,1)}, u32[]{:S(2)}, u32[]{:S(2)}) %all-to-all-start.1) | async-done | bytes 786464 | tf_op jit(solution)/shard_map/all_to_all | solution.py:17
  33.5 4.5 all-to-all-start
  38.7 15.8 %all-to-all-done = bf16[8,3,96,256]{3,2,1,0:T(8,128)(2,1)S(1)} async-done(((bf16[8,3,96,256]{3,2,1,0:T(8,128)(2,1)}), bf16[8,3,96,256]{3,2,1,0:T(8,128)(2,1)S(1)}, u32[]{:S(2)}, u32[]{:S(2)}) %all-to-all-start) | async-done | bytes 1179680 | tf_op jit(solution)/shard_map/all_to_all | solution.py:17
  57.2 74.6 %while.36 = (s32[]{:T(128)}, f32[16,96,256]{2,1,0:T(8,128)}, f32[24,96,256]{2,1,0:T(8,128)S(1)}, s32[]{:T(128)}, s32[128]{0:T(128)S(1)}, /*index=5*/s32[128]{0:T...) while((s32[]{:T(128)}, f32[16,96,256]{2,1,0:T(8,128)}, ...), condition=%wide.region_3.6_spmd, body=%wide.region_0.5_spmd.sunk | while | flops 202508432 | bytes 10758387 | solution.py:78
  63.0 1.8 gather_fusion
  66.6 3.0 scatter_fusion
  75.4 1.8 gather_fusion
  79.0 3.0 scatter_fusion
  87.9 1.8 gather_fusion
  91.4 3.1 scatter_fusion
  100.3 1.8 gather_fusion
  103.9 3.1 scatter_fusion
  112.9 1.8 gather_fusion
  116.4 3.0 scatter_fusion
  125.2 1.8 gather_fusion
  128.8 3.0 scatter_fusion
  131.8 33.7 %all_to_all.50 = f32[8,3,96,256]{3,2,1,0:T(8,128)} all-to-all(f32[8,3,96,256]{3,2,1,0:T(8,128)S(1)} %bitcast.64), channel_id=1, replica_groups=mesh['el_0'=4,'el_1'=2,'ph'=16] {'el_0','el_1'}, dimensions={0} | all-to-all | bytes 4718592 | tf_op jit(solution)/shard_map/all_to_all | solution.py:38
  165.5 115.4 %all-to-all-start.3 = ((f32[16,1,96,256]{3,2,1,0:T(8,128)}), f32[16,1,96,256]{3,2,1,0:T(8,128)}, u32[]{:S(2)}, u32[]{:S(2)}) async-start(f32[16,1,96,256]{3,2,1,0:T(8,128)} %bitcast.10), calls=%async_computation.3 | async-start | bytes 3145728 | tf_op jit(solution)/shard_map/all_to_all | solution.py:38
  281.2 21.5 %all_gather.12 = bf16[6,96,256]{2,1,0:T(8,128)(2,1)} all-gather(bf16[3,96,256]{2,1,0:T(8,128)(2,1)S(1)} %fusion.38), channel_id=1, replica_groups=mesh['el_0'=4,'el_1'=2,'ph'=16] {'el_1'}, dimensions={0}, use_global_device_ids=true | all-gather | bytes 442368 | tf_op jit(solution)/shard_map/all_gather | solution.py:45
  302.7 2.4 all-to-all-done.3
  307.6 5.6 all-to-all-start.4
  313.3 15.2 %all-to-all-done.4 = bf16[16,1,96,256]{3,2,1,0:T(8,128)(2,1)} async-done(((bf16[16,1,96,256]{3,2,1,0:T(8,128)(2,1)}), bf16[16,1,96,256]{3,2,1,0:T(8,128)(2,1)}, u32[]{:S(2)}, u32[]{:S(2)}) %all-to-all-start.4) | async-done | bytes 786464 | tf_op jit(solution)/shard_map/all_to_all | solution.py:17
  330.1 74.5 %while.37 = (s32[]{:T(128)}, f32[16,96,256]{2,1,0:T(8,128)}, f32[24,96,256]{2,1,0:T(8,128)S(1)}, s32[]{:T(128)}, s32[128]{0:T(128)S(1)}, /*index=5*/s32[128]{0:T...) while((s32[]{:T(128)}, f32[16,96,256]{2,1,0:T(8,128)}, ...), condition=%wide.region_9.12_spmd, body=%wide.region_6.11_spmd.sunk | while | flops 202508432 | bytes 10758387 | solution.py:78
  330.8 1.7 gather_fusion.3
  335.9 1.8 gather_fusion.2
  339.5 3.0 scatter_fusion.2
  343.1 1.7 gather_fusion.3
  348.3 1.8 gather_fusion.2
  351.9 3.0 scatter_fusion.2
  355.5 1.7 gather_fusion.3
  360.7 1.8 gather_fusion.2
  364.3 3.1 scatter_fusion.2
  368.0 1.7 gather_fusion.3
  373.2 1.8 gather_fusion.2
  376.7 3.1 scatter_fusion.2
  380.5 1.7 gather_fusion.3
  385.7 1.8 gather_fusion.2
  389.2 3.0 scatter_fusion.2
  392.9 1.7 gather_fusion.3
  398.1 1.8 gather_fusion.2
  401.6 3.0 scatter_fusion.2
  404.6 34.1 %all_to_all.51 = f32[8,3,96,256]{3,2,1,0:T(8,128)} all-to-all(f32[8,3,96,256]{3,2,1,0:T(8,128)S(1)} %bitcast.65), channel_id=1, replica_groups=mesh['el_0'=4,'el_1'=2,'ph'=16] {'el_0','el_1'}, dimensions={0} | all-to-all | bytes 4718592 | tf_op jit(solution)/shard_map/all_to_all | solution.py:38
  438.8 116.7 %all-to-all-start.6 = ((f32[16,1,96,256]{3,2,1,0:T(8,128)}), f32[16,1,96,256]{3,2,1,0:T(8,128)}, u32[]{:S(2)}, u32[]{:S(2)}) async-start(f32[16,1,96,256]{3,2,1,0:T(8,128)} %bitcast.16), calls=%async_computation.6 | async-start | bytes 3145728 | tf_op jit(solution)/shard_map/all_to_all | solution.py:38
  555.8 21.5 %all_gather.14 = bf16[6,96,256]{2,1,0:T(8,128)(2,1)} all-gather(bf16[3,96,256]{2,1,0:T(8,128)(2,1)S(1)} %fusion.40), channel_id=1, replica_groups=mesh['el_0'=4,'el_1'=2,'ph'=16] {'el_1'}, dimensions={0}, use_global_device_ids=true | all-gather | bytes 442368 | tf_op jit(solution)/shard_map/all_gather | solution.py:45
  577.3 2.4 all-to-all-done.6
  582.2 5.6 all-to-all-start.7
  587.9 15.1 %all-to-all-done.7 = bf16[16,1,96,256]{3,2,1,0:T(8,128)(2,1)S(1)} async-done(((bf16[16,1,96,256]{3,2,1,0:T(8,128)(2,1)}), bf16[16,1,96,256]{3,2,1,0:T(8,128)(2,1)S(1)}, u32[]{:S(2)}, u32[]{:S(2)}) %all-to-all-start.7) | async-done | bytes 786464 | tf_op jit(solution)/shard_map/all_to_all | solution.py:17
  604.8 68.1 %while.38 = (s32[]{:T(128)}, f32[16,96,256]{2,1,0:T(8,128)S(1)}, f32[24,96,256]{2,1,0:T(8,128)}, s32[]{:T(128)}, s32[128]{0:T(128)S(1)}, /*index=5*/s32[128]{0:T...) while((s32[]{:T(128)}, f32[16,96,256]{2,1,0:T(8,128)S(1)}, ...), condition=%wide.region_15.18_spmd, body=%wide.region_12.17_spmd.sunk | while | flops 202508432 | bytes 10758387 | solution.py:78
  608.4 3.1 scatter_fusion.5
  611.5 1.8 gather_fusion.4
  619.7 3.0 scatter_fusion.5
  622.8 1.8 gather_fusion.4
  631.1 3.1 scatter_fusion.5
  634.2 1.8 gather_fusion.4
  642.5 3.1 scatter_fusion.5
  645.6 1.8 gather_fusion.4
  653.9 3.1 scatter_fusion.5
  656.9 1.8 gather_fusion.4
  665.2 3.0 scatter_fusion.5
  668.2 1.8 gather_fusion.4
  673.0 136.5 %all_to_all.52 = f32[16,1,96,256]{3,2,1,0:T(8,128)} all-to-all(f32[16,1,96,256]{3,2,1,0:T(8,128)S(1)} %bitcast.63), channel_id=1, replica_groups=mesh['el_0'=4,'el_1'=2,'ph'=16] {'ph'}, dimensions={0} | all-to-all | bytes 3145728 | tf_op jit(solution)/shard_map/all_to_all | solution.py:38
  809.5 8.3 all-to-all-start.9
  820.1 27.0 %all-to-all-done.9 = f32[8,3,96,256]{3,2,1,0:T(8,128)S(1)} async-done(((f32[8,3,96,256]{3,2,1,0:T(8,128)}), f32[8,3,96,256]{3,2,1,0:T(8,128)S(1)}, u32[]{:S(2)}, u32[]{:S(2)}) %all-to-all-start.9) | async-done | bytes 2359328 | tf_op jit(solution)/shard_map/all_to_all | solution.py:38
  (243 shorter events, 135.8 us)
Async XLA Ops:
  7.2 10.0 %copy-start.9 = (f32[1,3,96,256]{3,2,1,0:T(8,128)S(1)}, f32[1,3,96,256]{3,2,1,0:T(8,128)}, u32[]{:S(2)}) copy-start(f32[1,3,96,256]{3,2,1,0:T(8,128)} %param.21) | copy-start | bytes 884740
  9.1 23.2 %all-to-all-start.1 = ((bf16[16,1,96,256]{3,2,1,0:T(8,128)(2,1)}), bf16[16,1,96,256]{3,2,1,0:T(8,128)(2,1)}, u32[]{:S(2)}, u32[]{:S(2)}) async-start(bf16[16,1,96,256]{3,2,1,0:T(8,128)(2,1)} %broadcast_in_dim.76), calls=%async_computation.1 | async-start | bytes 1572864 | tf_op jit(solution)/shard_map/all_to_all | solution.py:17
  33.5 21.1 %all-to-all-start = ((bf16[8,3,96,256]{3,2,1,0:T(8,128)(2,1)}), bf16[8,3,96,256]{3,2,1,0:T(8,128)(2,1)S(1)}, u32[]{:S(2)}, u32[]{:S(2)}) async-start(bf16[8,3,96,256]{3,2,1,0:T(8,128)(2,1)} %broadcast_in_dim.75), calls=%async_computation | async-start | bytes 2359296 | tf_op jit(solution)/shard_map/all_to_all | solution.py:17
  38.0 19.1 %copy-start.10 = (s32[1,1,128]{2,1,0:T(1,128)S(1)}, s32[1,1,128]{2,1,0:T(1,128)}, u32[]{:S(2)}) copy-start(s32[1,1,128]{2,1,0:T(1,128)} %param.27) | copy-start | bytes 1540
  38.0 19.1 %copy-start.11 = (s32[1,1,128]{2,1,0:T(1,128)S(1)}, s32[1,1,128]{2,1,0:T(1,128)}, u32[]{:S(2)}) copy-start(s32[1,1,128]{2,1,0:T(1,128)} %param.28) | copy-start | bytes 1540
  54.5 1.0 copy-start.2
  60.2 1.6 copy-start.15
  72.6 1.6 copy-start.15
  85.0 1.6 copy-start.15
  97.5 1.6 copy-start.15
  110.0 1.6 copy-start.15
  122.4 1.6 copy-start.15
  165.5 115.4 %copy-start.21 = (f32[1,3,256]{2,0,1:T(1,128)S(1)}, f32[1,3,256]{2,0,1:T(1,128)}, u32[]{:S(2)}) copy-start(f32[1,3,256]{2,0,1:T(1,128)} %param.25) | copy-start | bytes 9220
  165.5 115.4 %copy-start = (f32[8,3,96,256]{3,2,1,0:T(8,128)S(1)}, f32[8,3,96,256]{3,2,1,0:T(8,128)}, u32[]{:S(2)}) copy-start(f32[8,3,96,256]{3,2,1,0:T(8,128)} %all_to_all.50) | copy-start | bytes 7077892
  165.5 115.7 %copy-start.3 = (f32[1,3,96,256]{3,2,1,0:T(8,128)S(1)}, f32[1,3,96,256]{3,2,1,0:T(8,128)}, u32[]{:S(2)}) copy-start(f32[1,3,96,256]{3,2,1,0:T(8,128)} %param.23) | copy-start | bytes 884740
  165.5 139.6 %all-to-all-start.3 = ((f32[16,1,96,256]{3,2,1,0:T(8,128)}), f32[16,1,96,256]{3,2,1,0:T(8,128)}, u32[]{:S(2)}, u32[]{:S(2)}) async-start(f32[16,1,96,256]{3,2,1,0:T(8,128)} %bitcast.10), calls=%async_computation.3 | async-start | bytes 3145728 | tf_op jit(solution)/shard_map/all_to_all | solution.py:38
  280.9 47.6 %all-gather.3.cloned.1.call-start = ((), (), s32[]{:S(2)}) async-start(), calls=%async_computation.10 | async-start | bytes 1474560 | tf_op jit(solution)/shard_map/all_gather | solution.py:45
  280.9 25.7 %copy-start.12 = (f32[1,3,256]{2,1,0:T(4,128)}, f32[1,3,256]{2,1,0:T(4,128)S(1)}, u32[]{:S(2)}) copy-start(f32[1,3,256]{2,1,0:T(4,128)S(1)} %copy.14) | copy-start | bytes 9220
  281.0 25.7 %copy-start.6 = (f32[1,96,256]{2,1,0:T(8,128)S(1)}, f32[1,96,256]{2,1,0:T(8,128)}, u32[]{:S(2)}) copy-start(f32[1,96,256]{2,1,0:T(8,128)} %param.22) | copy-start | bytes 294916
  281.0 25.7 %copy-start.18 = (f32[1,256]{1,0:T(1,128)S(1)}, f32[1,256]{1,0:T(1,128)}, u32[]{:S(2)}) copy-start(f32[1,256]{1,0:T(1,128)} %param.24) | copy-start | bytes 3076
  307.6 20.9 %all-to-all-start.4 = ((bf16[16,1,96,256]{3,2,1,0:T(8,128)(2,1)}), bf16[16,1,96,256]{3,2,1,0:T(8,128)(2,1)}, u32[]{:S(2)}, u32[]{:S(2)}) async-start(bf16[16,1,96,256]{3,2,1,0:T(8,128)(2,1)} %broadcast_in_dim.77), calls=%async_computation.4 | async-start | bytes 1572864 | tf_op jit(solution)/shard_map/all_to_all | solution.py:17
  333.1 1.6 copy-start.16
  345.5 1.6 copy-start.16
  357.9 1.6 copy-start.16
  370.4 1.6 copy-start.16
  382.9 1.6 copy-start.16
  395.2 1.6 copy-start.16
  438.8 116.8 %copy-start.1 = (f32[8,3,96,256]{3,2,1,0:T(8,128)S(1)}, f32[8,3,96,256]{3,2,1,0:T(8,128)}, u32[]{:S(2)}) copy-start(f32[8,3,96,256]{3,2,1,0:T(8,128)} %all_to_all.51) | copy-start | bytes 7077892
  438.8 117.0 %copy-start.4 = (f32[1,3,96,256]{3,2,1,0:T(8,128)S(1)}, f32[1,3,96,256]{3,2,1,0:T(8,128)}, u32[]{:S(2)}) copy-start(f32[1,3,96,256]{3,2,1,0:T(8,128)} %param.23) | copy-start | bytes 884740
  438.8 117.0 %copy-start.13 = (f32[1,3,256]{2,1,0:T(4,128)S(1)}, f32[1,3,256]{2,1,0:T(4,128)}, u32[]{:S(2)}) copy-start(f32[1,3,256]{2,1,0:T(4,128)} %copy-done.12) | copy-start | bytes 9220
  438.8 141.0 %all-to-all-start.6 = ((f32[16,1,96,256]{3,2,1,0:T(8,128)}), f32[16,1,96,256]{3,2,1,0:T(8,128)}, u32[]{:S(2)}, u32[]{:S(2)}) async-start(f32[16,1,96,256]{3,2,1,0:T(8,128)} %bitcast.16), calls=%async_computation.6 | async-start | bytes 3145728 | tf_op jit(solution)/shard_map/all_to_all | solution.py:38
  555.5 25.7 %copy-start.7 = (f32[1,96,256]{2,1,0:T(8,128)S(1)}, f32[1,96,256]{2,1,0:T(8,128)}, u32[]{:S(2)}) copy-start(f32[1,96,256]{2,1,0:T(8,128)} %param.22) | copy-start | bytes 294916
  555.5 25.7 %copy-start.19 = (f32[1,256]{1,0:T(1,128)S(1)}, f32[1,256]{1,0:T(1,128)}, u32[]{:S(2)}) copy-start(f32[1,256]{1,0:T(1,128)} %param.24) | copy-start | bytes 3076
  555.5 47.5 %all-gather.5.cloned.1.call-start = ((), (), s32[]{:S(2)}) async-start(), calls=%async_computation.11 | async-start | bytes 1474560 | tf_op jit(solution)/shard_map/all_gather | solution.py:45
  582.2 20.8 %all-to-all-start.7 = ((bf16[16,1,96,256]{3,2,1,0:T(8,128)(2,1)}), bf16[16,1,96,256]{3,2,1,0:T(8,128)(2,1)S(1)}, u32[]{:S(2)}, u32[]{:S(2)}) async-start(bf16[16,1,96,256]{3,2,1,0:T(8,128)(2,1)} %broadcast_in_dim.78), calls=%async_computation.7 | async-start | bytes 1572864 | tf_op jit(solution)/shard_map/all_to_all | solution.py:17
  606.8 1.6 copy-start.17
  618.1 1.6 copy-start.17
  629.5 1.6 copy-start.17
  640.9 1.6 copy-start.17
  652.2 1.6 copy-start.17
  663.6 1.6 copy-start.17
  809.5 9.9 %copy-start.8 = (f32[1,96,256]{2,1,0:T(8,128)S(1)}, f32[1,96,256]{2,1,0:T(8,128)}, u32[]{:S(2)}) copy-start(f32[1,96,256]{2,1,0:T(8,128)} %param.22) | copy-start | bytes 294916
  809.5 9.9 %copy-start.20 = (f32[1,256]{1,0:T(1,128)S(1)}, f32[1,256]{1,0:T(1,128)}, u32[]{:S(2)}) copy-start(f32[1,256]{1,0:T(1,128)} %param.24) | copy-start | bytes 3076
  809.5 37.5 %all-to-all-start.9 = ((f32[8,3,96,256]{3,2,1,0:T(8,128)}), f32[8,3,96,256]{3,2,1,0:T(8,128)S(1)}, u32[]{:S(2)}, u32[]{:S(2)}) async-start(f32[8,3,96,256]{3,2,1,0:T(8,128)} %bitcast.66), calls=%async_computation.9 | async-start | bytes 4718592 | tf_op jit(solution)/shard_map/all_to_all | solution.py:38
  817.8 29.4 %copy-start.5 = (f32[1,3,96,256]{3,2,1,0:T(8,128)S(1)}, f32[1,3,96,256]{3,2,1,0:T(8,128)}, u32[]{:S(2)}) copy-start(f32[1,3,96,256]{3,2,1,0:T(8,128)} %param.23) | copy-start | bytes 884740
  817.8 29.4 %copy-start.14 = (f32[1,3,256]{2,1,0:T(4,128)S(1)}, f32[1,3,256]{2,1,0:T(4,128)}, u32[]{:S(2)}) copy-start(f32[1,3,256]{2,1,0:T(4,128)} %copy-done.12) | copy-start | bytes 9220
Sparse Core Ops, SparseCore 0:
  302.8 24.8 all-gather.2
  577.5 24.8 all-gather.4
where the time goes:
time: 865 us; the launch traced here: 855 us
  starting transfers between devices  264 us (31%)
  blocking collectives  247 us (29%)
  other arithmetic  107 us (12%)
  waiting for transfers between devices  93.1 us (11%)
  local copies, waits for them, and re-layouts  67.3 us (8%)
  matrix products  58.9 us (7%)
  between operations  15.1 us (2%)
    all_to_all x3, starting transfers between devices, summed_on_arrival(): lax.all_to_all(tiles, axis, split_axis=0, concat_axis=0, tiled=True)  240 us
    all_to_all x3, blocking collectives, summed_on_arrival(): lax.all_to_all(tiles, axis, split_axis=0, concat_axis=0, tiled=True)  204 us
    all_to_all x4, waiting for transfers between devices, copy_for_each(): return lax.all_to_all(copies, axis, split_axis=0, concat_axis=0, tiled=True)  61.3 us
    scatter-add x18, other arithmetic, one_group(): elec_total = elec_total.at[group_rows].add(to_electron)  43.4 us
    all_gather x2, blocking collectives, gather_axes(): nearer = lax.all_gather(shard, axes[-1], axis=dim, tiled=True)  43 us
    gather x18, local copies, waits for them, and re-layouts, one_group(): phon_in = jnp.take(phon_blocks, group_cols, axis=0)  33.2 us
    scatter-add x18, other arithmetic, one_group(): phon_total = phon_total.at[group_cols].add(to_phonon)  32.7 us
    all_to_all x3, waiting for transfers between devices, summed_on_arrival(): lax.all_to_all(tiles, axis, split_axis=0, concat_axis=0, tiled=True)  31.7 us
  transfers between devices with their start and end apart: 9, of which 7 were waited for; matrix products, arithmetic and copies ran while one was open for 1% of the time, Pallas kernels for 0%

commit v1 on v0

v1 whole, which is shorter than its diff:
```python
import jax
import jax.numpy as jnp
from jax import lax
from jax.experimental import pallas as pl
from jax.experimental.pallas import tpu as pltpu
from jax.sharding import Mesh
from jax.sharding import PartitionSpec as P

ITERS = 3
EL = ("el_0", "el_1")
EL_PH = ("el_0", "el_1", "ph")
UNROLL = 8
LOADS = 8


def copy_for_each(shard, axis):
    copies = jnp.broadcast_to(shard, (lax.axis_size(axis), *shard.shape))
    return lax.all_to_all(copies, axis, split_axis=0, concat_axis=0, tiled=True)


def gather_directly(shard, axis):
    blocks = copy_for_each(shard, axis)
    return blocks.reshape(-1, *shard.shape[1:])


def summed_on_arrival(shard, axis):
    size = lax.axis_size(axis)
    pieces = shard.reshape(size, -1, *shard.shape[1:])
    arrived = lax.all_to_all(pieces, axis, split_axis=0, concat_axis=0, tiled=True)
    return arrived.sum(axis=0)


def by_block(own, other, live_count, blocks):
    slots = own.shape[0]
    places = jnp.arange(slots, dtype=jnp.int32)
    live = places < live_count
    key = jnp.where(live, own, blocks) * slots + places
    rank = jnp.sum((key[None, :] < key[:, None]).astype(jnp.int32), axis=1)
    chosen = rank[None, :] == places[:, None]

    def sorted_as(values):
        return jnp.sum(jnp.where(chosen, values[None, :], 0), axis=1)

    order = sorted_as(places)
    partner = sorted_as(jnp.where(live, other, 0))
    block = sorted_as(jnp.where(live, own, blocks))
    before = jnp.concatenate([jnp.full((1,), -1, jnp.int32), block[:-1]])
    keep = (block == before).astype(jnp.float32)
    ids = jnp.arange(blocks, dtype=jnp.int32)
    up_to = jnp.sum(((own[None, :] <= ids[:, None]) & live[None, :]).astype(jnp.int32), axis=1)
    own_number = jnp.sum(((own[None, :] == ids[:, None]) & live[None, :]).astype(jnp.int32), axis=1)
    return order, partner, keep, jnp.maximum(up_to - 1, 0), jnp.minimum(own_number, 1).astype(jnp.float32)


def pass_kernel(
    p_order, p_other, p_keep, p_last, p_any, e_order, e_other, e_keep, e_last, e_any,
    tiles_hbm, elec, phon, elec_drag, phon_drag, tiles, partial, sems,
):
    slots = tiles.shape[0]
    part = slots // LOADS
    copies = [
        pltpu.make_async_copy(tiles_hbm.at[pl.ds(part * i, part)], tiles.at[pl.ds(part * i, part)], sems.at[i])
        for i in range(LOADS)
    ]
    for copy in copies:
        copy.start()
    for copy in copies:
        copy.wait()

    def run(order, other, keep, source, contract):
        def steps(group, total):
            for step in range(UNROLL):
                place = group * UNROLL + step
                product = lax.dot_general(
                    source[other[place]],
                    tiles[order[place]],
                    (((1,), (contract,)), ((), ())),
                    preferred_element_type=jnp.float32,
                )
                total = total * keep[place] + product
                partial[place] = total
            return total

        lax.fori_loop(0, slots // UNROLL, steps, jnp.zeros(partial.shape[1:], jnp.float32))

    run(p_order, p_other, p_keep, elec, 0)
    for block in range(phon_drag.shape[0]):
        phon_drag[block] = partial[p_last[block]] * p_any[block]
    run(e_order, e_other, e_keep, phon, 1)
    for block in range(elec_drag.shape[0]):
        elec_drag[block] = partial[e_last[block]] * e_any[block]


def tile_pass(tables, tile_set, elec_blocks, phon_blocks):
    vmem = pl.BlockSpec(memory_space=pltpu.VMEM)
    slots, side, _ = tile_set.shape
    rhs = elec_blocks.shape[1]
    return pl.pallas_call(
        pass_kernel,
        out_shape=(
            jax.ShapeDtypeStruct(elec_blocks.shape, jnp.float32),
            jax.ShapeDtypeStruct(phon_blocks.shape, jnp.float32),
        ),
        in_specs=[pl.BlockSpec(memory_space=pltpu.SMEM)] * 10
        + [pl.BlockSpec(memory_space=pl.ANY), vmem, vmem],
        out_specs=(vmem, vmem),
        scratch_shapes=[
            pltpu.VMEM((slots, side, side), jnp.bfloat16),
            pltpu.VMEM((slots, rhs, side), jnp.float32),
            pltpu.SemaphoreType.DMA((LOADS,)),
        ],
        compiler_params=pltpu.CompilerParams(vmem_limit_bytes=44 * 2**20),
        cost_estimate=pl.CostEstimate(
            flops=4 * slots * rhs * side * side, bytes_accessed=2 * slots * side * side, transcendentals=0
        ),
        name="tile_pass",
    )(*tables, tile_set, elec_blocks, phon_blocks)


def local(
    elec_dev, phon_dev, elec_source, phon_source, elec_rate, phon_rate, tiles, tile_rows, tile_cols, tile_count
):
    rows, cols, count = tile_rows[0, 0], tile_cols[0, 0], tile_count[0, 0]
    elec_range = gather_directly(elec_dev.astype(jnp.bfloat16), "ph")
    phon_range = gather_directly(phon_dev[0].astype(jnp.bfloat16), EL)
    tables = by_block(cols, rows, count, phon_range.shape[0]) + by_block(rows, cols, count, elec_range.shape[0])
    elec_now, phon_now = elec_dev, phon_dev[0]
    for sweep in range(ITERS):
        elec_drag, phon_drag = tile_pass(tables, tiles[0, 0], elec_range, phon_range)
        elec_now = (elec_source + summed_on_arrival(elec_drag, "ph")) / elec_rate[:, None, :]
        phon_now = (phon_source[0] + summed_on_arrival(phon_drag, EL)) / phon_rate[0][:, None, :]
        if sweep + 1 < ITERS:
            elec_range = gather_directly(elec_now.astype(jnp.bfloat16), "ph")
            phon_range = gather_directly(phon_now.astype(jnp.bfloat16), EL)
    return elec_now, phon_now[None]


def solution(mesh):
    split = Mesh(mesh.devices.reshape(4, 2, mesh.shape["ph"]), EL_PH)
    placed = (
        P(EL_PH, None, None),
        P("ph", EL, None, None),
        P(EL_PH, None, None),
        P("ph", EL, None, None),
        P(EL_PH, None),
        P("ph", EL, None),
        P(EL, "ph", None, None, None),
        P(EL, "ph", None),
        P(EL, "ph", None),
        P(EL, "ph"),
    )
    return jax.shard_map(
        local,
        mesh=split,
        in_specs=placed,
        out_specs=(P(EL_PH, None, None), P("ph", EL, None, None)),
        check_vma=False,
    )
```

time: 865 us -> 372 us (0.43); the launches traced: 855 us -> 371 us
  starting transfers between devices: 264 us -> 32.2 us
  blocking collectives: 247 us -> 121 us
  other arithmetic: 107 us -> 9.22 us
  local copies, waits for them, and re-layouts: 67.3 us -> 5.07 us
  Pallas kernels: 0 us -> 60.2 us
  matrix products: 58.9 us -> 0 us
  waiting for transfers between devices: 93.1 us -> 141 us
  between operations: 15.1 us -> 1.54 us
    all_to_all x3, starting transfers between devices: 240 us -> 12.3 us  [summed_on_arrival(): lax.all_to_all(pieces, axis, split_axis=0, concat_axis=0, tiled=True)]
    all_to_all x3 -> x5, blocking collectives: 204 us -> 121 us  [the longest x3 82.3 us: summed_on_arrival(): lax.all_to_all(pieces, axis, split_axis=0, concat_axis=0, tiled=True)]
    scatter-add x36 -> x0, other arithmetic: 76 us -> none  [the longest x18 43.4 us: one_group(): elec_total = elec_total.at[group_rows].add(to_electron)]
    pallas_call x0 -> x3, Pallas kernels: none -> 60.2 us  [tile_pass(): pl.pallas_call(pass_kernel, out_shape=(jax.ShapeDtypeStruct(elec_blocks.s...]
    dot_general x36 -> x0, matrix products: 58.9 us -> none  [the longest x18 30.4 us: one_group(): jnp.einsum('tkb,tab->tka', phon_in, block_tiles, preferred_element_type=j...]
    gather x36 -> x0, local copies, waits for them, and re-layouts: 57 us -> none  [the longest x18 33.2 us: one_group(): phon_in = jnp.take(phon_blocks, group_cols, axis=0)]
    all_to_all x3, waiting for transfers between devices: 31.7 us -> 85.2 us  [summed_on_arrival(): lax.all_to_all(pieces, axis, split_axis=0, concat_axis=0, tiled=True)]
    all_gather x2 -> x0, blocking collectives: 43 us -> none  [gather_axes(): nearer = lax.all_gather(shard, axes[-1], axis=dim, tiled=True)]
  transfers between devices with their start and end apart: 9 -> 7, of which waited for: 7 -> 7; matrix products, arithmetic and copies ran while one was open for 1% -> 2% of each run, Pallas kernels for 0% -> 0%
where the time goes in v1:
time: 372 us; the launch traced here: 371 us
  waiting for transfers between devices  141 us (38%)
  blocking collectives  121 us (33%)
  Pallas kernels  60.2 us (16%)
  starting transfers between devices  32.2 us (9%)
  other arithmetic  9.22 us (2%)
  local copies, waits for them, and re-layouts  5.07 us (1%)
    all_to_all x3, waiting for transfers between devices, summed_on_arrival(): lax.all_to_all(pieces, axis, split_axis=0, concat_axis=0, tiled=True)  85.2 us
    all_to_all x3, blocking collectives, summed_on_arrival(): lax.all_to_all(pieces, axis, split_axis=0, concat_axis=0, tiled=True)  82.3 us
    pallas_call x3, Pallas kernels, tile_pass(): pl.pallas_call(pass_kernel, out_shape=(jax.ShapeDtypeStruct(elec_blocks.s...  60.2 us
    all_to_all x4, waiting for transfers between devices, copy_for_each(): return lax.all_to_all(copies, axis, split_axis=0, concat_axis=0, tiled=True)  56.2 us
    all_to_all x2, blocking collectives, copy_for_each(): return lax.all_to_all(copies, axis, split_axis=0, concat_axis=0, tiled=True)  38.6 us
    all_to_all x4, starting transfers between devices, copy_for_each(): return lax.all_to_all(copies, axis, split_axis=0, concat_axis=0, tiled=True)  19.8 us
    all_to_all x3, starting transfers between devices, summed_on_arrival(): lax.all_to_all(pieces, axis, split_axis=0, concat_axis=0, tiled=True)  12.3 us
  transfers between devices with their start and end apart: 7, of which 7 were waited for; matrix products, arithmetic and copies ran while one was open for 2% of the time, Pallas kernels for 0%

profile of v1, /device:TPU:0, one launch (start us, length us, event | category | flops | bytes accessed | tf_op | source)
XLA Modules:
  0.0 370.5 jit_solution(15186560107886379269)
XLA Ops:
  0.6 0.0 copy-start.7
  0.6 0.0 copy-start.6
  0.7 0.0 copy-start.3
  0.7 0.9 convert_bitcast_fusion.1
  1.6 1.0 broadcast_in_dim.109
  2.6 8.0 %all-to-all-start = ((bf16[16,1,96,256]{3,2,1,0:T(8,128)(2,1)}), bf16[16,1,96,256]{3,2,1,0:T(8,128)(2,1)S(1)}, u32[]{:S(2)}, u32[]{:S(2)}) async-start(bf16[16,1,96,256]{3,2,1,0:T(8,128)(2,1)} %broadcast_in_dim.109), calls=%async_computation | async-start | bytes 1572864 | tf_op jit(solution)/shard_map/all_to_all | solution.py:18
  11.2 0.0 copy-done.7
  11.2 0.0 copy-done.6
  11.3 0.1 convert_reduce_fusion.2
  11.4 0.2 convert_reduce_fusion.1
  11.5 0.2 convert_reduce_fusion
  11.7 0.2 select_reduce_fusion.3
  11.9 0.0 copy-done.3
  11.9 13.8 %all-to-all-done = bf16[16,1,96,256]{3,2,1,0:T(8,128)(2,1)S(1)} async-done(((bf16[16,1,96,256]{3,2,1,0:T(8,128)(2,1)}), bf16[16,1,96,256]{3,2,1,0:T(8,128)(2,1)S(1)}, u32[]{:S(2)}, u32[]{:S(2)}) %all-to-all-start) | async-done | bytes 786464 | tf_op jit(solution)/shard_map/all_to_all | solution.py:18
  25.7 1.1 broadcast_in_dim.110
  26.8 4.5 %all-to-all-start.1 = ((bf16[8,3,96,256]{3,2,1,0:T(8,128)(2,1)}), bf16[8,3,96,256]{3,2,1,0:T(8,128)(2,1)S(1)}, u32[]{:S(2)}, u32[]{:S(2)}) async-start(bf16[8,3,96,256]{3,2,1,0:T(8,128)(2,1)} %broadcast_in_dim.110), calls=%async_computation.1 | async-start | bytes 2359296 | tf_op jit(solution)/shard_map/all_to_all | solution.py:18
  31.4 0.1 convert_reduce_fusion.4
  31.5 0.1 select_reduce_fusion
  31.6 0.1 compare_convert_fusion.1.p_keep
  31.7 0.1 compare_convert_fusion.e_keep
  31.8 16.1 %all-to-all-done.1 = bf16[8,3,96,256]{3,2,1,0:T(8,128)(2,1)S(1)} async-done(((bf16[8,3,96,256]{3,2,1,0:T(8,128)(2,1)}), bf16[8,3,96,256]{3,2,1,0:T(8,128)(2,1)S(1)}, u32[]{:S(2)}, u32[]{:S(2)}) %all-to-all-start.1) | async-done | bytes 1179680 | tf_op jit(solution)/shard_map/all_to_all | solution.py:18
  47.9 19.1 %tile_pass.3 = (f32[16,96,256]{2,1,0:T(8,128)S(1)}, f32[24,96,256]{2,1,0:T(8,128)S(1)}) custom-call(s32[128]{0:T(128)S(1)} %get-tuple-element.23.p_order, s32[128]{0:T(128)S(1)} %get-tuple-element.22.p_other, f32[128]{0:T(128)S(1)} %compare_convert_fusion.1.p_keep, s32[24]{0:T(128)S(1)} %get-tuple-element.34.p_last, f32[24]{0:T(128)S(1)} %get-tuple-element.33.p_any, ...), custom_call_target="tpu_custom_call" | custom-call | flops 3221225472 | bytes 16777216 | tf_op jit(solution)/shard_map/tile_pass/pallas_call | solution.py:98
  67.0 0.0 copy-start
  67.1 27.6 %all_to_all.60 = f32[16,1,96,256]{3,2,1,0:T(8,128)S(1)} all-to-all(f32[16,1,96,256]{3,2,1,0:T(8,128)S(1)} %bitcast.87), channel_id=1, replica_groups=mesh['el_0'=4,'el_1'=2,'ph'=16] {'ph'}, dimensions={0} | all-to-all | bytes 3145728 | tf_op jit(solution)/shard_map/all_to_all | solution.py:29
  94.7 0.0 copy-done
  94.7 4.4 %all-to-all-start.4 = ((f32[8,3,96,256]{3,2,1,0:T(8,128)}), f32[8,3,96,256]{3,2,1,0:T(8,128)}, u32[]{:S(2)}, u32[]{:S(2)}) async-start(f32[8,3,96,256]{3,2,1,0:T(8,128)} %bitcast.85), calls=%async_computation.4 | async-start | bytes 4718592 | tf_op jit(solution)/shard_map/all_to_all | solution.py:29
  99.1 0.0 copy-start.2
  99.1 0.0 copy-start.4
  99.1 0.1 reduce_sum.182
  99.2 0.0 copy-start.5
  99.2 0.8 copy-done.2
  100.0 0.0 copy-done.4
  100.0 28.6 %all-to-all-done.4 = f32[8,3,96,256]{3,2,1,0:T(8,128)} async-done(((f32[8,3,96,256]{3,2,1,0:T(8,128)}), f32[8,3,96,256]{3,2,1,0:T(8,128)}, u32[]{:S(2)}, u32[]{:S(2)}) %all-to-all-start.4) | async-done | bytes 2359328 | tf_op jit(solution)/shard_map/all_to_all | solution.py:29
  128.6 1.0 broadcast_in_dim.111
  129.5 3.7 all-to-all-start.3
  133.2 0.0 copy-done.5
  133.2 0.0 copy-start.1
  133.2 1.9 reduce_sum.184
  135.1 0.0 copy-done.1
  135.1 0.1 fusion.2
  135.2 13.1 %all-to-all-done.3 = bf16[16,1,96,256]{3,2,1,0:T(8,128)(2,1)S(1)} async-done(((bf16[16,1,96,256]{3,2,1,0:T(8,128)(2,1)}), bf16[16,1,96,256]{3,2,1,0:T(8,128)(2,1)S(1)}, u32[]{:S(2)}, u32[]{:S(2)}) %all-to-all-start.3) | async-done | bytes 786464 | tf_op jit(solution)/shard_map/all_to_all | solution.py:18
  148.3 0.1 broadcast_in_dim.112
  148.5 19.3 %all_to_all.61 = bf16[8,3,96,256]{3,2,1,0:T(8,128)(2,1)S(1)} all-to-all(bf16[8,3,96,256]{3,2,1,0:T(8,128)(2,1)S(1)} %broadcast_in_dim.112), channel_id=1, replica_groups=mesh['el_0'=4,'el_1'=2,'ph'=16] {'el_0','el_1'}, dimensions={0} | all-to-all | bytes 2359296 | tf_op jit(solution)/shard_map/all_to_all | solution.py:18
  167.8 20.5 %tile_pass.4 = (f32[16,96,256]{2,1,0:T(8,128)S(1)}, f32[24,96,256]{2,1,0:T(8,128)}) custom-call(s32[128]{0:T(128)S(1)} %get-tuple-element.23.p_order, s32[128]{0:T(128)S(1)} %get-tuple-element.22.p_other, f32[128]{0:T(128)S(1)} %compare_convert_fusion.1.p_keep, s32[24]{0:T(128)S(1)} %get-tuple-element.34.p_last, f32[24]{0:T(128)S(1)} %get-tuple-element.33.p_any, ...), custom_call_target="tpu_custom_call" | custom-call | flops 3221225472 | bytes 16777216 | tf_op jit(solution)/shard_map/tile_pass/pallas_call | solution.py:98
  188.3 27.3 %all_to_all.62 = f32[16,1,96,256]{3,2,1,0:T(8,128)S(1)} all-to-all(f32[16,1,96,256]{3,2,1,0:T(8,128)S(1)} %bitcast.88), channel_id=1, replica_groups=mesh['el_0'=4,'el_1'=2,'ph'=16] {'ph'}, dimensions={0} | all-to-all | bytes 3145728 | tf_op jit(solution)/shard_map/all_to_all | solution.py:29
  215.6 4.4 %all-to-all-start.8 = ((f32[8,3,96,256]{3,2,1,0:T(8,128)}), f32[8,3,96,256]{3,2,1,0:T(8,128)}, u32[]{:S(2)}, u32[]{:S(2)}) async-start(f32[8,3,96,256]{3,2,1,0:T(8,128)} %bitcast.22), calls=%async_computation.8 | async-start | bytes 4718592 | tf_op jit(solution)/shard_map/all_to_all | solution.py:29
  219.9 0.1 reduce_sum.185
  220.1 29.4 %all-to-all-done.8 = f32[8,3,96,256]{3,2,1,0:T(8,128)} async-done(((f32[8,3,96,256]{3,2,1,0:T(8,128)}), f32[8,3,96,256]{3,2,1,0:T(8,128)}, u32[]{:S(2)}, u32[]{:S(2)}) %all-to-all-start.8) | async-done | bytes 2359328 | tf_op jit(solution)/shard_map/all_to_all | solution.py:29
  249.4 1.0 broadcast_in_dim.113
  250.4 3.7 all-to-all-start.7
  254.1 1.9 reduce_sum.187
  255.9 0.1 fusion.4
  256.0 13.2 %all-to-all-done.7 = bf16[16,1,96,256]{3,2,1,0:T(8,128)(2,1)S(1)} async-done(((bf16[16,1,96,256]{3,2,1,0:T(8,128)(2,1)}), bf16[16,1,96,256]{3,2,1,0:T(8,128)(2,1)S(1)}, u32[]{:S(2)}, u32[]{:S(2)}) %all-to-all-start.7) | async-done | bytes 786464 | tf_op jit(solution)/shard_map/all_to_all | solution.py:18
  269.2 0.1 broadcast_in_dim.114
  269.3 19.3 %all_to_all.63 = bf16[8,3,96,256]{3,2,1,0:T(8,128)(2,1)S(1)} all-to-all(bf16[8,3,96,256]{3,2,1,0:T(8,128)(2,1)S(1)} %broadcast_in_dim.114), channel_id=1, replica_groups=mesh['el_0'=4,'el_1'=2,'ph'=16] {'el_0','el_1'}, dimensions={0} | all-to-all | bytes 2359296 | tf_op jit(solution)/shard_map/all_to_all | solution.py:18
  288.6 20.5 %tile_pass.5 = (f32[16,96,256]{2,1,0:T(8,128)S(1)}, f32[24,96,256]{2,1,0:T(8,128)}) custom-call(s32[128]{0:T(128)S(1)} %get-tuple-element.23.p_order, s32[128]{0:T(128)S(1)} %get-tuple-element.22.p_other, f32[128]{0:T(128)S(1)} %compare_convert_fusion.1.p_keep, s32[24]{0:T(128)S(1)} %get-tuple-element.34.p_last, f32[24]{0:T(128)S(1)} %get-tuple-element.33.p_any, ...), custom_call_target="tpu_custom_call" | custom-call | flops 3221225472 | bytes 16777216 | tf_op jit(solution)/shard_map/tile_pass/pallas_call | solution.py:98
  309.2 27.4 %all_to_all.64 = f32[16,1,96,256]{3,2,1,0:T(8,128)} all-to-all(f32[16,1,96,256]{3,2,1,0:T(8,128)S(1)} %bitcast.86), channel_id=1, replica_groups=mesh['el_0'=4,'el_1'=2,'ph'=16] {'ph'}, dimensions={0} | all-to-all | bytes 3145728 | tf_op jit(solution)/shard_map/all_to_all | solution.py:29
  336.6 3.6 all-to-all-start.11
  340.2 1.5 reduce_sum.188
  341.7 0.7 fusion.5
  342.4 27.2 %all-to-all-done.11 = f32[8,3,96,256]{3,2,1,0:T(8,128)S(1)} async-done(((f32[8,3,96,256]{3,2,1,0:T(8,128)}), f32[8,3,96,256]{3,2,1,0:T(8,128)S(1)}, u32[]{:S(2)}, u32[]{:S(2)}) %all-to-all-start.11) | async-done | bytes 2359328 | tf_op jit(solution)/shard_map/all_to_all | solution.py:29
  369.6 0.2 reduce_sum.190
  369.8 0.8 fusion
  (8 shorter events, 0.1 us)
Async XLA Ops:
  0.6 10.6 %copy-start.7 = (s32[1,1,128]{2,1,0:T(1,128)S(1)}, s32[1,1,128]{2,1,0:T(1,128)}, u32[]{:S(2)}) copy-start(s32[1,1,128]{2,1,0:T(1,128)} %param.17) | copy-start | bytes 1540
  0.6 10.6 %copy-start.6 = (s32[1,1,128]{2,1,0:T(1,128)S(1)}, s32[1,1,128]{2,1,0:T(1,128)}, u32[]{:S(2)}) copy-start(s32[1,1,128]{2,1,0:T(1,128)} %param.18) | copy-start | bytes 1540
  0.7 11.2 %copy-start.3 = (f32[1,3,96,256]{3,2,1,0:T(8,128)S(1)}, f32[1,3,96,256]{3,2,1,0:T(8,128)}, u32[]{:S(2)}) copy-start(f32[1,3,96,256]{3,2,1,0:T(8,128)} %param.11) | copy-start | bytes 884740
  2.6 23.1 %all-to-all-start = ((bf16[16,1,96,256]{3,2,1,0:T(8,128)(2,1)}), bf16[16,1,96,256]{3,2,1,0:T(8,128)(2,1)S(1)}, u32[]{:S(2)}, u32[]{:S(2)}) async-start(bf16[16,1,96,256]{3,2,1,0:T(8,128)(2,1)} %broadcast_in_dim.109), calls=%async_computation | async-start | bytes 1572864 | tf_op jit(solution)/shard_map/all_to_all | solution.py:18
  26.8 21.1 %all-to-all-start.1 = ((bf16[8,3,96,256]{3,2,1,0:T(8,128)(2,1)}), bf16[8,3,96,256]{3,2,1,0:T(8,128)(2,1)S(1)}, u32[]{:S(2)}, u32[]{:S(2)}) async-start(bf16[8,3,96,256]{3,2,1,0:T(8,128)(2,1)} %broadcast_in_dim.110), calls=%async_computation.1 | async-start | bytes 2359296 | tf_op jit(solution)/shard_map/all_to_all | solution.py:18
  67.0 27.6 %copy-start = (f32[24,96,256]{2,1,0:T(8,128)}, f32[24,96,256]{2,1,0:T(8,128)S(1)}, u32[]{:S(2)}) copy-start(f32[24,96,256]{2,1,0:T(8,128)S(1)} %get-tuple-element.9) | copy-start | bytes 7077892
  94.7 33.9 %all-to-all-start.4 = ((f32[8,3,96,256]{3,2,1,0:T(8,128)}), f32[8,3,96,256]{3,2,1,0:T(8,128)}, u32[]{:S(2)}, u32[]{:S(2)}) async-start(f32[8,3,96,256]{3,2,1,0:T(8,128)} %bitcast.85), calls=%async_computation.4 | async-start | bytes 4718592 | tf_op jit(solution)/shard_map/all_to_all | solution.py:29
  99.1 0.9 copy-start.2
  99.1 0.9 copy-start.4
  99.2 34.0 %copy-start.5 = (f32[1,3,256]{2,0,1:T(1,128)S(1)}, f32[1,3,256]{2,0,1:T(1,128)}, u32[]{:S(2)}) copy-start(f32[1,3,256]{2,0,1:T(1,128)} %param.15) | copy-start | bytes 9220
  129.5 18.8 %all-to-all-start.3 = ((bf16[16,1,96,256]{3,2,1,0:T(8,128)(2,1)}), bf16[16,1,96,256]{3,2,1,0:T(8,128)(2,1)S(1)}, u32[]{:S(2)}, u32[]{:S(2)}) async-start(bf16[16,1,96,256]{3,2,1,0:T(8,128)(2,1)} %broadcast_in_dim.111), calls=%async_computation.3 | async-start | bytes 1572864 | tf_op jit(solution)/shard_map/all_to_all | solution.py:18
  133.2 1.9 copy-start.1
  215.6 33.9 %all-to-all-start.8 = ((f32[8,3,96,256]{3,2,1,0:T(8,128)}), f32[8,3,96,256]{3,2,1,0:T(8,128)}, u32[]{:S(2)}, u32[]{:S(2)}) async-start(f32[8,3,96,256]{3,2,1,0:T(8,128)} %bitcast.22), calls=%async_computation.8 | async-start | bytes 4718592 | tf_op jit(solution)/shard_map/all_to_all | solution.py:29
  250.4 18.8 %all-to-all-start.7 = ((bf16[16,1,96,256]{3,2,1,0:T(8,128)(2,1)}), bf16[16,1,96,256]{3,2,1,0:T(8,128)(2,1)S(1)}, u32[]{:S(2)}, u32[]{:S(2)}) async-start(bf16[16,1,96,256]{3,2,1,0:T(8,128)(2,1)} %broadcast_in_dim.113), calls=%async_computation.7 | async-start | bytes 1572864 | tf_op jit(solution)/shard_map/all_to_all | solution.py:18
  336.6 33.0 %all-to-all-start.11 = ((f32[8,3,96,256]{3,2,1,0:T(8,128)}), f32[8,3,96,256]{3,2,1,0:T(8,128)S(1)}, u32[]{:S(2)}, u32[]{:S(2)}) async-start(f32[8,3,96,256]{3,2,1,0:T(8,128)} %bitcast.27), calls=%async_computation.11 | async-start | bytes 4718592 | tf_op jit(solution)/shard_map/all_to_all | solution.py:29

commit v2 on v1

v2 whole, which is shorter than its diff:
```python
import jax
import jax.numpy as jnp
from jax import lax
from jax.experimental import pallas as pl
from jax.experimental.pallas import tpu as pltpu
from jax.sharding import PartitionSpec as P

ITERS = 3
UNROLL = 8
LOADS = 8
TOP = 32000.0
FINE = 8.0
MESH = pl.DeviceIdType.MESH


def by_block(own, other, live_count, blocks):
    slots = own.shape[0]
    places = jnp.arange(slots, dtype=jnp.int32)
    live = places < live_count
    key = jnp.where(live, own, blocks) * slots + places
    rank = jnp.sum((key[None, :] < key[:, None]).astype(jnp.int32), axis=1)
    chosen = rank[None, :] == places[:, None]

    def sorted_as(values):
        return jnp.sum(jnp.where(chosen, values[None, :], 0), axis=1)

    order = sorted_as(places)
    partner = sorted_as(jnp.where(live, other, 0))
    block = sorted_as(jnp.where(live, own, blocks))
    before = jnp.concatenate([jnp.full((1,), -1, jnp.int32), block[:-1]])
    keep = (block == before).astype(jnp.float32)
    ids = jnp.arange(blocks, dtype=jnp.int32)
    up_to = jnp.sum(((own[None, :] <= ids[:, None]) & live[None, :]).astype(jnp.int32), axis=1)
    own_number = jnp.sum(((own[None, :] == ids[:, None]) & live[None, :]).astype(jnp.int32), axis=1)
    return order, partner, keep, jnp.maximum(up_to - 1, 0), jnp.minimum(own_number, 1).astype(jnp.float32)


(AX, AYP, AYM, AHP, AHM, AQP, AQM, AOX) = range(8)
(R8, R6, R7, R4, R5, R1, R2, R3) = range(8, 16)
GE = 16
SE = 31
MESSAGES = 39


def kernel(
    p_order, p_other, p_keep, p_last, p_any, e_order, e_other, e_keep, e_last, e_any,
    tiles_hbm, elec_dev, phon_dev, elec_source, phon_source, elec_rate, phon_rate,
    elec_out, phon_out,
    tiles, seg_p, seg_e, pb, eb, psend, precv, dsend, drecv, esend, erecv, tmp,
    load_sems, send_sems, recv_sems,
):
    slots = tiles.shape[0]
    part = slots // LOADS
    loads = [
        pltpu.make_async_copy(tiles_hbm.at[pl.ds(part * i, part)], tiles.at[pl.ds(part * i, part)], load_sems.at[i])
        for i in range(LOADS)
    ]
    for load in loads:
        load.start()

    el, ph = lax.axis_index("el"), lax.axis_index("ph")
    y, xl = lax.div(el, 2), lax.rem(el, 2)
    yp, ym, yo, xq = lax.rem(y + 1, 4), lax.rem(y + 3, 4), lax.rem(y + 2, 4), 1 - xl
    xh, z, core = lax.div(ph, 8), lax.rem(lax.div(ph, 2), 4), lax.rem(ph, 2)
    zp, zm, zo, hq = lax.rem(z + 1, 4), lax.rem(z + 3, 4), lax.rem(z + 2, 4), 1 - xh

    def at_y(yy, xx):
        return 2 * yy + xx

    def at_z(hh, zz, cc):
        return 8 * hh + 2 * zz + cc

    p_x, p_yp, p_ym = (at_y(y, xq), ph), (at_y(yp, xl), ph), (at_y(ym, xl), ph)
    sib = (el, at_z(xh, z, 1 - core))
    e_zp, e_zm, e_zo, e_x = (
        (el, at_z(xh, zp, core)),
        (el, at_z(xh, zm, core)),
        (el, at_z(xh, zo, core)),
        (el, at_z(hq, z, core)),
    )

    barrier = pltpu.get_barrier_semaphore()
    for peer in (p_x, p_yp, p_ym, sib, e_zp, e_zm, e_zo, e_x):
        pl.semaphore_signal(barrier, inc=1, device_id=peer, device_id_type=MESH)
    pl.semaphore_wait(barrier, 8)

    def message(s, i, src, dst, peer):
        return pltpu.make_async_remote_copy(
            src_ref=src,
            dst_ref=dst,
            send_sem=send_sems.at[s, i],
            recv_sem=recv_sems.at[s, i],
            device_id=peer,
            device_id_type=MESH,
        )

    def unit(s, yy, xx):
        return pb.at[s, pl.ds(3 * at_y(yy, xx), 3)]

    def half(s, yy, xx, h):
        return pb.at[s, pl.ds(3 * at_y(yy, xx), 3), pl.ds(48 * h, 48)]

    def gather_p(s):
        def pair(i, peer, sent, got):
            return (lambda: message(s, i, sent, sent, peer)), (lambda: message(s, i, got, got, peer))

        return {
            AX: pair(AX, p_x, unit(s, y, xl), unit(s, y, xq)),
            AYP: pair(AYP, p_yp, unit(s, y, xl), unit(s, ym, xl)),
            AYM: pair(AYM, p_ym, unit(s, y, xl), unit(s, yp, xl)),
            AHP: pair(AHP, p_yp, half(s, ym, xl, 0), half(s, yo, xl, 0)),
            AHM: pair(AHM, p_ym, half(s, yp, xl, 1), half(s, yo, xl, 1)),
            AQP: pair(AQP, p_yp, unit(s, y, xq), unit(s, ym, xq)),
            AQM: pair(AQM, p_ym, unit(s, y, xq), unit(s, yp, xq)),
            AOX: pair(AOX, p_x, unit(s, yo, xl), unit(s, yo, xq)),
        }

    def eblock(s, hh, zz, cc):
        return eb.at[s, at_z(hh, zz, cc)]

    def gather_e(s):
        def pair(i, peer, sent, got):
            return (lambda: message(s, i, sent, sent, peer)), (lambda: message(s, i, got, got, peer))

        out = {}
        for k, (peer, came) in enumerate(((e_x, None), (e_zp, zm), (e_zm, zp), (e_zo, zo))):
            if came is None:
                out[k] = pair(GE + k, peer, eblock(s, xh, z, core), eblock(s, hq, z, core))
            else:
                out[k] = pair(GE + k, peer, eblock(s, xh, z, core), eblock(s, xh, came, core))
                out[k + 3] = pair(GE + k + 3, peer, eblock(s, hq, z, core), eblock(s, hq, came, core))
        for k, (hh, zz) in enumerate(
            ((xh, z), (hq, z), (xh, zm), (xh, zp), (xh, zo), (hq, zm), (hq, zp), (hq, zo))
        ):
            out[7 + k] = pair(GE + 7 + k, sib, eblock(s, hh, zz, core), eblock(s, hh, zz, 1 - core))
        return out

    def send(table, *ids):
        for i in ids:
            table[i][0]().start()

    def got(table, *ids):
        for i in ids:
            table[i][1]().wait_recv()

    def sent(table):
        for out, _ in table.values():
            out().wait_send()

    def start_gather_p(s):
        send(gather_p(s), AX, AYP, AYM)

    def start_gather_e(s):
        send(gather_e(s), 0, 1, 2, 3, 7)

    def finish_gathers(s):
        p, e = gather_p(s), gather_e(s)
        got(e, 0)
        send(e, 4, 5, 6, 8)
        got(e, 1, 2)
        send(e, 9, 10)
        got(p, AYP)
        send(p, AHP)
        got(p, AYM)
        send(p, AHM)
        got(p, AX)
        send(p, AQP, AQM)
        got(e, 3)
        send(e, 11)
        got(e, 4, 5)
        send(e, 12, 13)
        got(e, 6)
        send(e, 14)
        got(p, AHP, AHM)
        send(p, AOX)
        got(e, 7, 8, 9, 10, 11, 12, 13, 14)
        got(p, AQP, AQM, AOX)
        sent(e)
        sent(p)

    def run(order, other, keep, source, contract, partial):
        def steps(group, total):
            for step in range(UNROLL):
                place = group * UNROLL + step
                product = lax.dot_general(
                    source[other[place]],
                    tiles[order[place]],
                    (((1,), (contract,)), ((), ())),
                    preferred_element_type=jnp.float32,
                )
                total = total * keep[place] + product
                partial[place] = total
            return total

        lax.fori_loop(0, slots // UNROLL, steps, jnp.zeros(partial.shape[1:], jnp.float32))

    def own_p(u):
        def value(i, k):
            block = 3 * u + lax.div(i, 2)
            rows = pl.ds(pl.multiple_of(48 * lax.rem(i, 2) + 16 * k, 16), 16)
            return seg_p[p_last[block], rows, :] * p_any[block]

        return value

    def own_e(block):
        def value(i, k):
            rows = pl.ds(pl.multiple_of(48 * i + 16 * k, 16), 16)
            return seg_e[e_last[block], rows, :] * e_any[block]

        return value

    def scale_of(ref, scale_row):
        coded = ref[scale_row : scale_row + 16, :].astype(jnp.int32).astype(jnp.float32)
        return jnp.exp2(coded * (1.0 / FINE)) * (1.0 / TOP)

    def over(pieces, carry, own, scale_row, extra, visit):
        for shift, first, end, refs in pieces:
            scales = [scale_of(ref, scale_row) for ref in refs]

            def body(i, carry, shift=shift, refs=refs, scales=scales):
                for k in range(3):
                    row = pl.multiple_of(48 * i + 16 * k, 16)
                    value = own(i, k)
                    if extra is not None:
                        value = value + extra(i, k)
                    for ref, scale in zip(refs, scales):
                        coded = ref[pl.ds(pl.multiple_of(row + shift, 16), 16), :]
                        value = value + coded.astype(jnp.int32).astype(jnp.float32) * scale
                    carry = visit(row, i, k, value, carry)
                return carry

            carry = lax.fori_loop(first, end, body, carry)
        return carry

    def code(out, pieces, own, scale_row, extra=None):
        def keep_it(row, i, k, value, most):
            tmp[pl.ds(row, 16), :] = value
            return jnp.maximum(most, jnp.abs(value))

        most = over(pieces, jnp.zeros((16, tmp.shape[1]), jnp.float32), own, scale_row, extra, keep_it)
        level = jnp.ceil(jnp.log2(jnp.maximum(most, 1e-30)) * FINE)
        out[scale_row : scale_row + 16, :] = level.astype(jnp.int32).astype(jnp.int16)
        scale = jnp.exp2(level * (-1.0 / FINE)) * TOP
        for shift, first, end, _ in pieces:

            def body(i, carry, shift=shift):
                for k in range(3):
                    row = pl.multiple_of(48 * i + 16 * k, 16)
                    whole = jnp.round(tmp[pl.ds(row, 16), :] * scale).astype(jnp.int32)
                    out[pl.ds(pl.multiple_of(row + shift, 16), 16), :] = whole.astype(jnp.int16)
                return carry

            lax.fori_loop(first, end, body, 0)

    def code_p(slot, u, low=(), high=()):
        code(psend.at[slot], ((0, 0, 3, low), (16, 3, 6, high)), own_p(u), 144)

    def pair_e(s, hh, zz):
        value = own_e(at_z(hh, zz, core))
        k4 = 4 * hh + zz

        def both(i, k):
            rows = pl.ds(pl.multiple_of(48 * i + 16 * k, 16), 16)
            return value(i, k) + drecv[s, k4, rows, :]

        return both

    def code_e(s, slot, hh, zz, refs=()):
        code(esend.at[slot], ((0, 0, 2, refs),), pair_e(s, hh, zz), 96)

    pb[0, pl.ds(3 * el, 3)] = phon_dev[...].astype(jnp.bfloat16)
    start_gather_p(0)
    eb[0, ph] = elec_dev[...].astype(jnp.bfloat16)
    start_gather_e(0)
    finish_gathers(0)
    for load in loads:
        load.wait()

    def sweep(s, _):
        run(p_order, p_other, p_keep, eb.at[s], 0, seg_p)

        rp = {}

        def route(i, peer, src, dst):
            rp[i] = (lambda: message(s, i, src, dst, peer),) * 2

        route(R8, p_x, psend.at[0], precv.at[s, 0])
        route(R6, p_ym, psend.at[1], precv.at[s, 1])
        route(R7, p_yp, psend.at[2], precv.at[s, 2])
        route(R4, p_ym, psend.at[3, pl.ds(0, 160)], precv.at[s, 3, pl.ds(0, 160)])
        route(R5, p_yp, psend.at[3, pl.ds(144, 160)], precv.at[s, 7, pl.ds(144, 160)])
        route(R1, p_x, psend.at[4], precv.at[s, 4])
        route(R2, p_ym, psend.at[5], precv.at[s, 5])
        route(R3, p_yp, psend.at[6], precv.at[s, 6])

        re = {}

        def route_e(i, peer, src, dst):
            re[i] = (lambda: message(s, SE + i, src, dst, peer),) * 2

        route_e(7, sib, dsend, drecv.at[s])
        for i, peer in enumerate((e_zp, e_zm, e_zo, e_zp, e_zm, e_zo, e_x)):
            route_e(i, peer, esend.at[i], erecv.at[s, i])

        code_p(0, at_y(yo, xq))
        send(rp, R8)
        code_p(1, at_y(ym, xq))
        send(rp, R6)
        code_p(2, at_y(yp, xq))
        send(rp, R7)

        run(e_order, e_other, e_keep, pb.at[s], 1, seg_e)

        for k in range(8):
            block = at_z(k // 4, k % 4, 1 - core)
            dsend[k] = seg_e[e_last[block]] * e_any[block]
        send(re, 7)

        got(rp, R8)
        code_p(3, at_y(yo, xl), (precv.at[s, 0],), (precv.at[s, 0],))
        send(rp, R4, R5)
        got(rp, R6, R7)
        code_p(4, at_y(y, xq), (precv.at[s, 1], precv.at[s, 2]), (precv.at[s, 1], precv.at[s, 2]))
        send(rp, R1)

        got(re, 7)
        for i, (hh, zz) in enumerate(((hq, zp), (hq, zm), (hq, zo), (xh, zp), (xh, zm), (xh, zo))):
            code_e(s, i, hh, zz)
            send(re, i)

        got(rp, R4)
        code_p(5, at_y(ym, xl), (precv.at[s, 3],), ())
        send(rp, R2)
        got(rp, R5)
        code_p(6, at_y(yp, xl), (), (precv.at[s, 7],))
        send(rp, R3)

        got(re, 0, 1, 2)
        code_e(s, 6, hq, z, (erecv.at[s, 0], erecv.at[s, 1], erecv.at[s, 2]))
        send(re, 6)
        got(re, 3, 4, 5)

        got(rp, R1, R2, R3)
        arrived = tuple(precv.at[s, i] for i in (4, 5, 6))

        def new_p(row, i, k, value, carry):
            third = lax.div(i, 2)
            rows = pl.ds(pl.multiple_of(48 * lax.rem(i, 2) + 16 * k, 16), 16)
            phon_out[third, rows, :] = (phon_source[third, rows, :] + value) / phon_rate[third]
            return carry

        over(((0, 0, 3, arrived), (16, 3, 6, arrived)), 0, own_p(el), 144, None, new_p)

        @pl.when(s < ITERS - 1)
        def _():
            pb[s + 1, pl.ds(3 * el, 3)] = phon_out[...].astype(jnp.bfloat16)
            start_gather_p(s + 1)

        got(re, 6)
        arrived_e = tuple(erecv.at[s, i] for i in (3, 4, 5, 6))

        def new_e(row, i, k, value, carry):
            rows = pl.ds(row, 16)
            elec_out[rows, :] = (elec_source[rows, :] + value) / elec_rate[...]
            return carry

        over(((0, 0, 2, arrived_e),), 0, pair_e(s, xh, z), 96, None, new_e)
        sent(rp)
        sent(re)

        @pl.when(s < ITERS - 1)
        def _():
            eb[s + 1, ph] = elec_out[...].astype(jnp.bfloat16)
            start_gather_e(s + 1)
            finish_gathers(s + 1)

        return 0

    lax.fori_loop(0, ITERS, sweep, 0)


def local(
    elec_dev, phon_dev, elec_source, phon_source, elec_rate, phon_rate, tiles, tile_rows, tile_cols, tile_count
):
    rows, cols, count = tile_rows[0, 0], tile_cols[0, 0], tile_count[0, 0]
    tables = by_block(cols, rows, count, 24) + by_block(rows, cols, count, 16)
    slots, side, _ = tiles.shape[2:]
    rhs = elec_dev.shape[1]
    vmem = pl.BlockSpec(memory_space=pltpu.VMEM)
    elec_out, phon_out = pl.pallas_call(
        kernel,
        out_shape=(
            jax.ShapeDtypeStruct((rhs, side), jnp.float32),
            jax.ShapeDtypeStruct((3, rhs, side), jnp.float32),
        ),
        in_specs=[pl.BlockSpec(memory_space=pltpu.SMEM)] * 10 + [pl.BlockSpec(memory_space=pl.ANY)] + [vmem] * 6,
        out_specs=(vmem, vmem),
        scratch_shapes=[
            pltpu.VMEM((slots, side, side), jnp.bfloat16),
            pltpu.VMEM((slots, rhs, side), jnp.float32),
            pltpu.VMEM((slots, rhs, side), jnp.float32),
            pltpu.VMEM((ITERS, 24, rhs, side), jnp.bfloat16),
            pltpu.VMEM((ITERS, 16, rhs, side), jnp.bfloat16),
            pltpu.VMEM((7, 304, side), jnp.int16),
            pltpu.VMEM((ITERS, 8, 304, side), jnp.int16),
            pltpu.VMEM((8, rhs, side), jnp.float32),
            pltpu.VMEM((ITERS, 8, rhs, side), jnp.float32),
            pltpu.VMEM((7, 112, side), jnp.int16),
            pltpu.VMEM((ITERS, 7, 112, side), jnp.int16),
            pltpu.VMEM((288, side), jnp.float32),
            pltpu.SemaphoreType.DMA((LOADS,)),
            pltpu.SemaphoreType.DMA((ITERS, MESSAGES)),
            pltpu.SemaphoreType.DMA((ITERS, MESSAGES)),
        ],
        compiler_params=pltpu.CompilerParams(
            vmem_limit_bytes=62 * 2**20, collective_id=0, has_side_effects=True
        ),
        name="sweeps",
    )(
        *tables,
        tiles[0, 0],
        elec_dev[0],
        phon_dev[0],
        elec_source[0],
        phon_source[0],
        elec_rate,
        phon_rate[0][:, None, :],
    )
    return elec_out[None], phon_out[None]


def solution(mesh):
    both = ("el", "ph")
    placed = (
        P(both, None, None),
        P("ph", "el", None, None),
        P(both, None, None),
        P("ph", "el", None, None),
        P(both, None),
        P("ph", "el", None),
        P("el", "ph", None, None, None),
        P("el", "ph", None),
        P("el", "ph", None),
        P("el", "ph"),
    )
    return jax.shard_map(
        local,
        mesh=mesh,
        in_specs=placed,
        out_specs=(P(both, None, None), P("ph", "el", None, None)),
        check_vma=False,
    )
```

time: 372 us -> 138 us (0.37)
  waiting for transfers between devices: 141 us -> 0 us
  blocking collectives: 121 us -> 0 us
  Pallas kernels: 60.2 us -> 124 us
  starting transfers between devices: 32.2 us -> 0 us
    all_to_all x7 -> x0, waiting for transfers between devices: 141 us -> none  [the longest x3 85.2 us: summed_on_arrival(): lax.all_to_all(pieces, axis, split_axis=0, concat_axis=0, tiled=True)]
    all_to_all x5 -> x0, blocking collectives: 121 us -> none  [the longest x3 82.3 us: summed_on_arrival(): lax.all_to_all(pieces, axis, split_axis=0, concat_axis=0, tiled=True)]
    pallas_call x3 -> x1, Pallas kernels: 60.2 us -> 124 us  [local(): pl.pallas_call(kernel, out_shape=(jax.ShapeDtypeStruct((rhs, side), jnp.f...]
    all_to_all x7 -> x0, starting transfers between devices: 32.2 us -> none  [the longest x4 19.8 us: copy_for_each(): return lax.all_to_all(copies, axis, split_axis=0, concat_axis=0, tiled=True)]
    reduce_sum x6 -> x0, other arithmetic: 5.62 us -> none  [summed_on_arrival(): return arrived.sum(axis=0)]
    broadcast_in_dim x6 -> x0, local copies, waits for them, and re-layouts: 4.27 us -> none  [copy_for_each(): copies = jnp.broadcast_to(shard, (lax.axis_size(axis), *shard.shape))]
  transfers between devices with their start and end apart: 7 -> 0, of which waited for: 7 -> 0; matrix products, arithmetic and copies ran while one was open for 2% -> 0% of each run, Pallas kernels for 0% -> 0%
where the time goes in v2:
time: 138 us; the launch traced here: 135 us
  Pallas kernels  124 us (90%)
  other arithmetic  6.45 us (5%)
  local copies, waits for them, and re-layouts  3.23 us (2%)
    pallas_call x1, Pallas kernels, local(): pl.pallas_call(kernel, out_shape=(jax.ShapeDtypeStruct((rhs, side), jnp.f...  124 us
    unnamed x2, local copies, waits for them, and re-layouts  3.23 us

profile of v2, /device:TPU:0, one launch (start us, length us, event | category | flops | bytes accessed | tf_op | source)
XLA Modules:
  0.0 135.3 jit_solution(16479320710210722316)
XLA Ops:
  1.3 0.8 convert_reduce_fusion.2
  2.1 0.6 minimum_convert_fusion.1
  2.7 0.8 convert_reduce_fusion.4
  3.4 0.6 minimum_convert_fusion
  4.0 0.7 iota_add_fusion
  4.7 0.2 convert_reduce_fusion
  4.8 0.7 select_reduce_fusion
  5.6 0.7 compare_convert_fusion.e_keep
  6.2 0.2 convert_reduce_fusion.1
  6.4 0.7 select_reduce_fusion.3
  7.1 0.6 compare_convert_fusion.1.p_keep
  7.7 124.3 %sweeps.1 = (f32[96,256]{1,0:T(8,128)}, f32[3,96,256]{2,1,0:T(8,128)}) custom-call(s32[128]{0:T(128)} %get-tuple-element.15.p_order, s32[128]{0:T(128)} %get-tuple-element.14.p_other, f32[128]{0:T(128)} %compare_convert_fusion.1.p_keep, s32[24]{0:T(128)} %get-tuple-element.26.p_last, f32[24]{0:T(128)} %get-tuple-element.25.p_any, ...), custom_call_target="tpu_custom_call" | custom-call | tf_op jit(solution)/shard_map/sweeps/pallas_call | solution.py:390
  132.1 1.5 %copy.15 = f32[1,96,256]{2,1,0:T(8,128)} copy(f32[1,96,256]{2,1,0:T(8,128)} %bitcast.27) | data formatting | bytes 196608
  133.6 1.7 %copy.16 = f32[1,3,96,256]{3,2,1,0:T(8,128)} copy(f32[1,3,96,256]{3,2,1,0:T(8,128)} %bitcast.22) | data formatting | bytes 589824
  (1 shorter events, 0.0 us)

commit v3 on v1

v3 whole, which is shorter than its diff:
```python
import random

import jax
import jax.numpy as jnp
from jax import lax
from jax.experimental import pallas as pl
from jax.experimental.pallas import tpu as pltpu
from jax.sharding import PartitionSpec as P

ITERS = 3
UNROLL = 8
LOADS = 8
PIECES = 5
TOP = 32000.0
FINE = 8.0
MESH = pl.DeviceIdType.MESH

WIRE = 46.7e3
HOP = {"x": 1.9, "y+": 2.0, "y-": 2.0, "z+": 2.0, "z-": 2.0, "zz": 2.5, "xx": 2.5, "d": 0.9}
LINK = {"x": "x", "xx": "x", "y+": "y+", "y-": "y-", "z+": "z+", "z-": "z-", "zz": "z+", "d": "d"}
LOAD = {"xx": 1.2, "zz": 1.2, "d": 0.07}
PASSES = (("P", 0), ("E", 0), ("E", 1), ("P", 1), ("P", 2), ("E", 2))
SEED = 0
SPREAD = 0.0
P_HALF, P_CODED, E_BLOCK, E_CODED = 3 * 48 * 512, 160 * 512, 96 * 512, 112 * 512


class Plan:
    def __init__(self):
        self.steps = {}

    def add(self, name, cost, after=(), needs=(), sends=()):
        self.steps[name] = (cost, tuple(after), tuple(needs), tuple(sends))

    def order(self):
        chance = random.Random(SEED)
        lean = {n: chance.uniform(1.0 - SPREAD, 1.0 + SPREAD) for n in self.steps}
        sender = {m: (n, way, size) for n, (_, _, _, sends) in self.steps.items() for m, way, size in sends}
        users = {n: [] for n in self.steps}
        for name, (_, after, needs, _) in self.steps.items():
            for n in after:
                users[n].append((name, 0.0))
            for m in needs:
                n, way, size = sender[m]
                users[n].append((name, HOP[way] + size * LOAD.get(way, 1.0) / WIRE))
        tail = {}

        def rest(name):
            if name not in tail:
                cost = self.steps[name][0]
                tail[name] = cost + max((gap + rest(n) for n, gap in users[name]), default=0.0)
            return tail[name]

        now, free, arrival, done, result = 0.0, {}, {}, set(), []
        left = dict.fromkeys(self.steps)
        while left:
            ready = []
            for name in left:
                _, after, needs, _ = self.steps[name]
                if all(n in done for n in after) and all(m in arrival for m in needs):
                    urgent = 1000.0 if self.steps[name][0] < 0.04 else 0.0
                    ready.append((max([now] + [arrival[m] for m in needs]), -rest(name) * lean[name] - urgent, name))
            soonest = min(ready)[0]
            start, _, name = min((r for r in ready if r[0] <= max(now, soonest) + 0.05), key=lambda r: r[1])
            cost, _, _, sends = self.steps[name]
            now = start + cost
            for m, way, size in sends:
                link = LINK[way]
                begin = max(now, free.get(link, 0.0))
                free[link] = begin + size * LOAD.get(way, 1.0) / WIRE
                arrival[m] = free[link] + HOP[way]
            done.add(name)
            del left[name]
            result.append((name, start, now))
        return result


def plan():
    p = Plan()
    for s in range(ITERS):
        if s == 0:
            p.add(("put_e", 0), 0.05, (), (), e_first(0))
            for h in range(2):
                p.add(("put_p", 0, h), 0.05, (("put_e", 0),), (), p_first(0, h))
        own_p = [("put_p", s, h) for h in range(2)]
        for m, by, way, h in (("AHP", "AYP", "y+", 0), ("AHM", "AYM", "y-", 1)):
            p.add((m, s), 0.01, (), ((by, s, h),), (((m, s), way, P_HALF),))
        for h, by in ((0, "AHP"), (1, "AHM")):
            p.add(("AQ", s, h), 0.02, (), (("AX", s, h),), ((("AQP", s, h), "y+", P_HALF), (("AQM", s, h), "y-", P_HALF)))
            p.add(("AOX", s, h), 0.01, (), ((by, s),), ((("AOX", s, h), "x", P_HALF),))
        p.add(("F", s), 0.03, (), (("G", s, 0),), e_onward(s))
        for k, by in ((9, 1), (10, 2), (11, 3), (12, 4), (13, 5), (14, 6)):
            p.add(("S", s, k), 0.01, (), (("G", s, by),), ((("G", s, k), "d", E_BLOCK),))
        all_p = [(m, s, h) for m in ("AX", "AYP", "AYM", "AQP", "AQM", "AOX") for h in range(2)]
        all_p += [("AHP", s), ("AHM", s)]
        all_e = [("G", s, k) for k in range(15)]
        for k in range(PIECES):
            for way, arrived, extra in (("P", all_e, [("put_e", s)]), ("E", all_p, own_p)):
                if k:
                    p.add((way, s, k), (P_TIME if way == "P" else E_TIME) / PIECES, ((way, s, k - 1),))
                else:
                    old = [n for n in p.steps if n[1] == s - 1 and n[0] in (P_CODES if way == "P" else E_CODES)]
                    old = [n for n in old if n != ("T", s - 1, 6)]
                    if way == "P" and s:
                        old += own_p
                    p.add((way, s, k), (P_TIME if way == "P" else E_TIME) / PIECES, old + extra, arrived)
        last_p, last_e = (("P", s, PIECES - 1),), (("E", s, PIECES - 1),)
        for h in range(2):
            for m, way in (("R8", "x"), ("R6", "y-"), ("R7", "y+")):
                p.add((m, s, h), 0.13, last_p, (), (((m, s, h), way, P_CODED),))
        p.add(("R4", s, 0), 0.14, last_p, (("R8", s, 0),), ((("R4", s, 0), "y-", P_CODED),))
        p.add(("R5", s, 1), 0.14, last_p, (("R8", s, 1),), ((("R5", s, 1), "y+", P_CODED),))
        for h in range(2):
            p.add(("R1", s, h), 0.15, last_p, (("R6", s, h), ("R7", s, h)), ((("R1", s, h), "x", P_CODED),))
            low, high = ((("R4", s, 0),), ()) if h == 0 else ((), (("R5", s, 1),))
            p.add(("R2", s, h), 0.14, last_p + ((("R4", s, 0),) if h else ()), low, ((("R2", s, h), "y-", P_CODED),))
            p.add(("R3", s, h), 0.14, last_p + (() if h else (("R5", s, 1),)), high, ((("R3", s, h), "y+", P_CODED),))
            p.add(
                ("put_p", s + 1, h), 0.15, last_p, (("R1", s, h), ("R2", s, h), ("R3", s, h)),
                p_first(s + 1, h) if s + 1 < ITERS else (),
            )
        p.add(("D", s), 0.3, last_e, (), ((("D", s), "d", 16 * E_BLOCK),))
        for k, way in enumerate(("z+", "z-", "zz", "z+", "z-", "zz")):
            p.add(("T", s, k), 0.09, last_e, (("D", s),), ((("T", s, k), way, E_CODED),))
        before = (("put_e", s),)
        p.add(("K", s), 0.08, last_e + before, (("D", s),))
        p.add(("T", s, 6), 0.12, (("K", s),), [("T", s, k) for k in range(3)], ((("T", s, 6), "xx", E_CODED),))
        p.add(
            ("put_e", s + 1), 0.15, (("K", s), ("T", s, 6)), [("T", s, k) for k in range(3, 7)],
            e_first(s + 1) if s + 1 < ITERS else (),
        )
    for before, name in zip(PASSES, PASSES[1:]):
        cost, after, needs, sends = p.steps[name + (0,)]
        p.steps[name + (0,)] = (cost, after + (before + (PIECES - 1,),), needs, sends)
    return p


P_TIME, E_TIME = 5.1, 7.5
P_CODES, E_CODES = ("R8", "R6", "R7", "R4", "R5", "R1", "R2", "R3"), ("D", "T", "K")


def e_first(s):
    ways = ("xx", "z+", "z-", "zz")
    return tuple((("G", s, k), way, E_BLOCK) for k, way in enumerate(ways)) + ((("G", s, 7), "d", E_BLOCK),)


def e_onward(s):
    ways = ("z+", "z-", "zz")
    return tuple((("G", s, 4 + k), way, E_BLOCK) for k, way in enumerate(ways)) + ((("G", s, 8), "d", E_BLOCK),)


def p_first(s, h):
    return tuple(((m, s, h), way, P_HALF) for m, way in (("AX", "x"), ("AYP", "y+"), ("AYM", "y-")))


def tables_of(own, other, live, blocks, whole, parts):
    slots = own.shape[1]
    square = (slots, slots)
    here = lax.broadcasted_iota(jnp.int32, square, 1)
    there = lax.broadcasted_iota(jnp.int32, square, 0)

    def down(row):
        return jnp.broadcast_to(row, square).T

    block = jnp.where(live, own, blocks)
    key = block * slots + here[0:1]
    rank = jnp.sum((down(key) < key).astype(jnp.int32), axis=0, keepdims=True)
    place = down(rank)
    block_down = down(block)

    def moved(values, by):
        return jnp.sum(jnp.where(place + by == here, values, 0), axis=0, keepdims=True)

    whole[0:1, :] = moved(there, 0)
    whole[1:2, :] = moved(down(jnp.where(live, other, 0)), 0)
    up_to = jnp.sum((block_down <= here).astype(jnp.int32), axis=0, keepdims=True)
    whole[2:3, :] = jnp.maximum(jnp.where(here[0:1] < blocks, up_to, 1) - 1, 0)
    parts[0:1, :] = (moved(block_down + 1, 0) == moved(block_down + 1, 1)).astype(jnp.float32)
    has = jnp.sum((block_down == here).astype(jnp.int32), axis=0, keepdims=True)
    parts[1:2, :] = (has > 0).astype(jnp.float32)


PER_SWEEP = 51
P_SLOTS = {"R8": 0, "R6": 2, "R7": 4, "R4": 6, "R5": 6, "R1": 8, "R2": 10, "R3": 12}


def kernel(
    count, slot_rows, slot_cols, tiles_hbm, elec_dev, phon_dev, elec_source, phon_source, elec_rate, phon_rate,
    elec_out, phon_out,
    tiles, seg_p, seg_e, pb_0, pb_1, pb_2, eb_0, eb_1, eb_2, psend, precv, dsend, drecv, esend, erecv, kept, tmp,
    whole_v, parts_v, whole, parts, load_sems, table_sems, send_sems, recv_sems,
):
    pb, eb = (pb_0, pb_1, pb_2), (eb_0, eb_1, eb_2)
    slots = tiles.shape[0]
    part = slots // LOADS
    loads = [
        pltpu.make_async_copy(tiles_hbm.at[pl.ds(part * i, part)], tiles.at[pl.ds(part * i, part)], load_sems.at[i])
        for i in range(LOADS)
    ]
    el, ph = lax.axis_index("el"), lax.axis_index("ph")
    y, xl = lax.div(el, 2), lax.rem(el, 2)
    yp, ym, yo, xq = lax.rem(y + 1, 4), lax.rem(y + 3, 4), lax.rem(y + 2, 4), 1 - xl
    xh, z, core = lax.div(ph, 8), lax.rem(lax.div(ph, 2), 4), lax.rem(ph, 2)
    zp, zm, zo, hq = lax.rem(z + 1, 4), lax.rem(z + 3, 4), lax.rem(z + 2, 4), 1 - xh

    def at_y(yy, xx):
        return 2 * yy + xx

    def at_z(hh, zz, cc):
        return 8 * hh + 2 * zz + cc

    p_x, p_yp, p_ym = (at_y(y, xq), ph), (at_y(yp, xl), ph), (at_y(ym, xl), ph)
    sib = (el, at_z(xh, z, 1 - core))
    e_zp, e_zm, e_zo, e_x = (
        (el, at_z(xh, zp, core)),
        (el, at_z(xh, zm, core)),
        (el, at_z(xh, zo, core)),
        (el, at_z(hq, z, core)),
    )

    barrier = pltpu.get_barrier_semaphore()
    for peer in (p_x, p_yp, p_ym, sib, e_zp, e_zm, e_zo, e_x):
        pl.semaphore_signal(barrier, inc=1, device_id=peer, device_id_type=MESH)
    for load in loads:
        load.start()

    live = lax.broadcasted_iota(jnp.int32, (1, slots), 1) < count[0, 0]
    table_copies = []
    for i, (own, other, blocks) in enumerate(((slot_cols, slot_rows, 24), (slot_rows, slot_cols, 16))):
        tables_of(own[...], other[...], live, blocks, whole_v.at[i], parts_v.at[i])
    for i, (src, dst) in enumerate(((whole_v, whole), (parts_v, parts))):
        table_copies.append(pltpu.make_async_copy(src, dst, table_sems.at[i]))
        table_copies[-1].start()
    pl.semaphore_wait(barrier, 8)

    def unit(s, h, yy, xx):
        return pb[s].at[pl.ds(3 * at_y(yy, xx), 3), pl.ds(48 * h, 48)]

    def eblock(s, hh, zz, cc):
        return eb[s].at[at_z(hh, zz, cc)]

    mail = {}

    def route(key, peer, src, dst, got):
        mail[key] = (len(mail), src, dst, peer, got)

    for s in range(ITERS):
        for h in range(2):
            for name, peer, sent, got in (
                ("AX", p_x, (y, xl), (y, xq)),
                ("AYP", p_yp, (y, xl), (ym, xl)),
                ("AYM", p_ym, (y, xl), (yp, xl)),
                ("AQP", p_yp, (y, xq), (ym, xq)),
                ("AQM", p_ym, (y, xq), (yp, xq)),
                ("AOX", p_x, (yo, xl), (yo, xq)),
            ):
                route((name, s, h), peer, unit(s, h, *sent), unit(s, h, *sent), unit(s, h, *got))
            for name, peer in (
                ("R8", p_x), ("R6", p_ym), ("R7", p_yp), ("R1", p_x), ("R2", p_ym), ("R3", p_yp),
                ("R5" if h else "R4", p_yp if h else p_ym),
            ):
                slot = P_SLOTS[name] + h
                route((name, s, h), peer, psend.at[slot], precv.at[s, slot], precv.at[s, slot])
        route(("AHP", s), p_yp, unit(s, 0, ym, xl), unit(s, 0, ym, xl), unit(s, 0, yo, xl))
        route(("AHM", s), p_ym, unit(s, 1, yp, xl), unit(s, 1, yp, xl), unit(s, 1, yo, xl))
        own = eblock(s, xh, z, core)
        far = eblock(s, hq, z, core)
        route(("G", s, 0), e_x, own, own, far)
        for k, (peer, came) in enumerate(((e_zp, zm), (e_zm, zp), (e_zo, zo))):
            route(("G", s, 1 + k), peer, own, own, eblock(s, xh, came, core))
            route(("G", s, 4 + k), peer, far, far, eblock(s, hq, came, core))
        for k, at in enumerate(((xh, z), (hq, z), (xh, zm), (xh, zp), (xh, zo), (hq, zm), (hq, zp), (hq, zo))):
            route(("G", s, 7 + k), sib, eblock(s, *at, core), eblock(s, *at, core), eblock(s, *at, 1 - core))
        route(("D", s), sib, dsend, drecv.at[s], drecv.at[s])
        for k, peer in enumerate((e_zp, e_zm, e_zo, e_zp, e_zm, e_zo, e_x)):
            route(("T", s, k), peer, esend.at[k], erecv.at[s, k], erecv.at[s, k])

    def copy_of(key, arriving=False):
        place, src, dst, peer, got = mail[key]
        return pltpu.make_async_remote_copy(
            src_ref=got if arriving else src,
            dst_ref=got if arriving else dst,
            send_sem=send_sems.at[place],
            recv_sem=recv_sems.at[place],
            device_id=peer,
            device_id_type=MESH,
        )

    leaving, waited = [], set()

    def send(*keys):
        for key in keys:
            copy_of(key).start()
            leaving.append(key)

    def left(key):
        if key in leaving:
            copy_of(key).wait_send()
            leaving.remove(key)

    def run(way, s, piece):
        table, source, contract, partial = (0, eb[s], 0, seg_p) if way == "P" else (1, pb[s], 1, seg_e)
        groups = slots // UNROLL
        first, end = (-(-groups * k // PIECES) for k in (piece, piece + 1))

        def steps(group, total):
            for step in range(UNROLL):
                place = group * UNROLL + step
                product = lax.dot_general(
                    source[whole[table, 1, place]],
                    tiles[whole[table, 0, place]],
                    (((1,), (contract,)), ((), ())),
                    preferred_element_type=jnp.float32,
                )
                total = total * parts[table, 0, place] + product
                partial[place] = total
            return total

        start = partial[first * UNROLL - 1] if piece else jnp.zeros(partial.shape[1:], jnp.float32)
        lax.fori_loop(first, end, steps, start)

    def own_p(u, h):
        def value(i, k):
            block = 3 * u + i
            return seg_p[whole[0, 2, block], pl.ds(48 * h + 16 * k, 16), :] * parts[0, 1, block]

        return value

    def rows_of(i, k):
        return pl.ds(pl.multiple_of(48 * i + 16 * k, 16), 16)

    def own_e(block):
        def value(i, k):
            return seg_e[whole[1, 2, block], rows_of(i, k), :] * parts[1, 1, block]

        return value

    def pair_e(s, hh, zz):
        value = own_e(at_z(hh, zz, core))
        place = 4 * hh + zz
        return lambda i, k: value(i, k) + drecv[s, place, rows_of(i, k), :]

    def kept_e(place):
        return lambda i, k: kept[place, rows_of(i, k), :]

    def scale_of(ref, pieces):
        coded = ref[48 * pieces : 48 * pieces + 16, :].astype(jnp.int32).astype(jnp.float32)
        return jnp.exp2(coded * (1.0 / FINE)) * (1.0 / TOP)

    def over(pieces, carry, own, refs, visit):
        scales = [scale_of(ref, pieces) for ref in refs]

        def body(i, carry):
            for k in range(3):
                value = own(i, k)
                for ref, scale in zip(refs, scales):
                    value = value + ref[rows_of(i, k), :].astype(jnp.int32).astype(jnp.float32) * scale
                carry = visit(i, k, value, carry)
            return carry

        return lax.fori_loop(0, pieces, body, carry)

    def code(out, pieces, own, refs):
        def keep_it(i, k, value, most):
            tmp[rows_of(i, k), :] = value
            return jnp.maximum(most, jnp.abs(value))

        most = over(pieces, jnp.zeros((16, tmp.shape[1]), jnp.float32), own, refs, keep_it)
        level = jnp.ceil(jnp.log2(jnp.maximum(most, 1e-30)) * FINE)
        out[48 * pieces : 48 * pieces + 16, :] = level.astype(jnp.int32).astype(jnp.int16)
        scale = jnp.exp2(level * (-1.0 / FINE)) * TOP

        def body(i, carry):
            for k in range(3):
                out[rows_of(i, k), :] = jnp.round(tmp[rows_of(i, k), :] * scale).astype(jnp.int32).astype(jnp.int16)
            return carry

        lax.fori_loop(0, pieces, body, 0)

    owner_p = {
        "R8": (yo, xq), "R6": (ym, xq), "R7": (yp, xq), "R4": (yo, xl), "R5": (yo, xl),
        "R1": (y, xq), "R2": (ym, xl), "R3": (yp, xl),
    }
    owner_e = ((hq, zp), (hq, zm), (hq, zo), (xh, zp), (xh, zm), (xh, zo), (hq, z))

    def put_p(s, h, needs):
        if s == 0:
            pb[0][pl.ds(3 * el, 3), 48 * h : 48 * h + 48] = phon_dev[:, 48 * h : 48 * h + 48].astype(jnp.bfloat16)
            return

        def visit(i, k, value, carry):
            rows = pl.ds(48 * h + 16 * k, 16)
            total = phon_source[i, rows, :] + value
            if s < ITERS:
                pb[s][3 * el + i, rows, :] = (total / phon_rate[i]).astype(jnp.bfloat16)
            else:
                phon_out[i, rows, :] = total
            return carry

        over(3, 0, own_p(el, h), [mail[m][4] for m in needs], visit)

    def put_e(s, needs):
        if s == 0:
            eb[0][ph] = elec_dev[...].astype(jnp.bfloat16)
            return

        def visit(i, k, value, carry):
            rows = rows_of(i, k)
            total = elec_source[rows, :] + value
            if s < ITERS:
                eb[s][ph, rows, :] = (total / elec_rate[...]).astype(jnp.bfloat16)
            else:
                elec_out[rows, :] = total
            return carry

        over(2, 0, kept_e(0), [mail[m][4] for m in needs], visit)

    steps = plan()
    loaded = False
    for name, _, _ in steps.order():
        _, _, needs, sends = steps.steps[name]
        for m in needs:
            if m not in waited:
                copy_of(m, arriving=True).wait_recv()
                waited.add(m)
        kind, s = name[:2]
        if kind in ("P", "E"):
            if not loaded:
                for copy in table_copies + loads:
                    copy.wait()
                loaded = True
            run(kind, s, name[2])
        elif kind == "put_p":
            put_p(s, name[2], needs)
        elif kind == "put_e":
            put_e(s, needs)
        elif kind in P_SLOTS:
            h = name[2]
            left((kind, s - 1, h))
            code(psend.at[P_SLOTS[kind] + h], 3, own_p(at_y(*owner_p[kind]), h), [mail[m][4] for m in needs])
        elif kind == "D":
            left(("D", s - 1))
            for k in range(8):
                block = at_z(k // 4, k % 4, 1 - core)
                dsend[k] = seg_e[whole[1, 2, block]] * parts[1, 1, block]
        elif kind == "K":
            for k, hh in enumerate((xh, hq)):
                block = at_z(hh, z, core)
                kept[k] = seg_e[whole[1, 2, block]] * parts[1, 1, block] + drecv[s, 4 * hh + z]
        elif kind == "T":
            k = name[2]
            left(("T", s - 1, k))
            code(esend.at[k], 2, kept_e(1) if k == 6 else pair_e(s, *owner_e[k]), [mail[m][4] for m in needs if k == 6])
        send(*(m for m, _, _ in sends))
    for key in tuple(leaving):
        left(key)


def local(
    elec_dev, phon_dev, elec_source, phon_source, elec_rate, phon_rate, tiles, tile_rows, tile_cols, tile_count
):
    slots, side, _ = tiles.shape[2:]
    rhs = elec_dev.shape[1]
    vmem, smem = pl.BlockSpec(memory_space=pltpu.VMEM), pl.BlockSpec(memory_space=pltpu.SMEM)
    elec_sum, phon_sum = pl.pallas_call(
        kernel,
        out_shape=(
            jax.ShapeDtypeStruct((rhs, side), jnp.float32),
            jax.ShapeDtypeStruct((3, rhs, side), jnp.float32),
        ),
        in_specs=[smem, vmem, vmem, pl.BlockSpec(memory_space=pl.ANY)] + [vmem] * 6,
        out_specs=(vmem, vmem),
        scratch_shapes=[
            pltpu.VMEM((slots, side, side), jnp.bfloat16),
            pltpu.VMEM((slots, rhs, side), jnp.float32),
            pltpu.VMEM((slots, rhs, side), jnp.float32),
            *[pltpu.VMEM((24, rhs, side), jnp.bfloat16)] * ITERS,
            *[pltpu.VMEM((16, rhs, side), jnp.bfloat16)] * ITERS,
            pltpu.VMEM((14, 160, side), jnp.int16),
            pltpu.VMEM((ITERS, 14, 160, side), jnp.int16),
            pltpu.VMEM((8, rhs, side), jnp.float32),
            pltpu.VMEM((ITERS, 8, rhs, side), jnp.float32),
            pltpu.VMEM((7, 112, side), jnp.int16),
            pltpu.VMEM((ITERS, 7, 112, side), jnp.int16),
            pltpu.VMEM((2, rhs, side), jnp.float32),
            pltpu.VMEM((144, side), jnp.float32),
            pltpu.VMEM((2, 8, slots), jnp.int32),
            pltpu.VMEM((2, 8, slots), jnp.float32),
            pltpu.SMEM((2, 8, slots), jnp.int32),
            pltpu.SMEM((2, 8, slots), jnp.float32),
            pltpu.SemaphoreType.DMA((LOADS,)),
            pltpu.SemaphoreType.DMA((2,)),
            pltpu.SemaphoreType.DMA((ITERS * PER_SWEEP,)),
            pltpu.SemaphoreType.DMA((ITERS * PER_SWEEP,)),
        ],
        compiler_params=pltpu.CompilerParams(
            vmem_limit_bytes=62 * 2**20, collective_id=0, has_side_effects=True
        ),
        name="sweeps",
    )(
        tile_count,
        tile_rows[0],
        tile_cols[0],
        tiles[0, 0],
        elec_dev[0],
        phon_dev[0],
        elec_source[0],
        phon_source[0],
        elec_rate,
        phon_rate[0][:, None, :],
    )
    return elec_sum[None] / elec_rate[:, None, :], phon_sum[None] / phon_rate[:, :, None, :]


def solution(mesh):
    both = ("el", "ph")
    placed = (
        P(both, None, None),
        P("ph", "el", None, None),
        P(both, None, None),
        P("ph", "el", None, None),
        P(both, None),
        P("ph", "el", None),
        P("el", "ph", None, None, None),
        P("el", "ph", None),
        P("el", "ph", None),
        P("el", "ph"),
    )
    return jax.shard_map(
        local,
        mesh=mesh,
        in_specs=placed,
        out_specs=(P(both, None, None), P("ph", "el", None, None)),
        check_vma=False,
    )
```

time: 372 us -> 120 us (0.32)
  waiting for transfers between devices: 141 us -> 0 us
  blocking collectives: 121 us -> 0 us
  Pallas kernels: 60.2 us -> 115 us
  starting transfers between devices: 32.2 us -> 0 us
  other arithmetic: 9.22 us -> 3.25 us
  local copies, waits for them, and re-layouts: 5.07 us -> 0.69 us
    all_to_all x7 -> x0, waiting for transfers between devices: 141 us -> none  [the longest x3 85.2 us: summed_on_arrival(): lax.all_to_all(pieces, axis, split_axis=0, concat_axis=0, tiled=True)]
    all_to_all x5 -> x0, blocking collectives: 121 us -> none  [the longest x3 82.3 us: summed_on_arrival(): lax.all_to_all(pieces, axis, split_axis=0, concat_axis=0, tiled=True)]
    pallas_call x3 -> x1, Pallas kernels: 60.2 us -> 115 us  [local(): pl.pallas_call(kernel, out_shape=(jax.ShapeDtypeStruct((rhs, side), jnp.f...]
    all_to_all x7 -> x0, starting transfers between devices: 32.2 us -> none  [the longest x4 19.8 us: copy_for_each(): return lax.all_to_all(copies, axis, split_axis=0, concat_axis=0, tiled=True)]
    reduce_sum x12 -> x0, other arithmetic: 6.51 us -> none  [the longest x6 5.62 us: summed_on_arrival(): return arrived.sum(axis=0)]
    broadcast_in_dim x6 -> x0, local copies, waits for them, and re-layouts: 4.27 us -> none  [copy_for_each(): copies = jnp.broadcast_to(shard, (lax.axis_size(axis), *shard.shape))]
  transfers between devices with their start and end apart: 7 -> 0, of which waited for: 7 -> 0; matrix products, arithmetic and copies ran while one was open for 2% -> 0% of each run, Pallas kernels for 0% -> 0%
where the time goes in v3:
time: 120 us
  Pallas kernels  115 us (96%)
  other arithmetic  3.25 us (3%)
  between operations  1.31 us (1%)
    pallas_call x1, Pallas kernels, local(): pl.pallas_call(kernel, out_shape=(jax.ShapeDtypeStruct((rhs, side), jnp.f...  115 us

profile of v3, /device:TPU:0, one launch (start us, length us, event | category | flops | bytes accessed | tf_op | source)
XLA Modules:
  0.0 119.8 jit_solution(12971670740897439678)
XLA Ops:
  0.6 0.0 copy-start
  1.3 0.7 copy.14
  2.0 114.5 %sweeps.1 = (f32[96,256]{1,0:T(8,128)}, f32[3,96,256]{2,1,0:T(8,128)}) custom-call(s32[1,1]{1,0:T(1,128)S(6)} %copy.15.count, s32[1,128]{1,0:T(1,128)} %bitcast.24, s32[1,128]{1,0:T(1,128)} %bitcast.25, bf16[128,256,256]{2,1,0:T(8,128)(2,1)} %bitcast.16, f32[96,256]{1,0:T(8,128)} %bitcast.19, f32[3,96,256]{2,1,0:T(8,128)} %bitcast.17, f32[96,256]{1,0:T(8,128)} %bitcast.20, ...), custom_call_target="tpu_custom_call" | custom-call | tf_op jit(solution)/shard_map/sweeps/pallas_call | solution.py:465
  116.5 0.0 copy-done
  116.5 1.5 %divide_bitcast_fusion.1 = f32[1,96,256]{2,1,0:T(8,128)} fusion(f32[96,256]{1,0:T(8,128)} %get-tuple-element.4, f32[256]{0:T(256)S(1)} %bitcast.23), kind=kLoop, calls=%fused_computation.1 | loop fusion | flops 24576 | bytes 197632 | tf_op jit(solution)/shard_map/div | solution.py:512
  118.1 1.7 %divide_bitcast_fusion = f32[1,3,96,256]{3,2,1,0:T(8,128)} fusion(f32[3,96,256]{2,1,0:T(8,128)} %get-tuple-element.5, f32[3,256]{1,0:T(4,128)S(1)} %bitcast.21), kind=kLoop, calls=%fused_computation | loop fusion | flops 73728 | bytes 592896 | tf_op jit(solution)/shard_map/div | solution.py:512
Async XLA Ops:
  0.6 115.9 %copy-start = (f32[1,256]{1,0:T(1,128)S(1)}, f32[1,256]{1,0:T(1,128)}, u32[]{:S(2)}) copy-start(f32[1,256]{1,0:T(1,128)} %elec_rate.1) | copy-start | bytes 3076

commit v4 on v3

--- a/solution.py
+++ b/solution.py
@@ -186,7 +186,7 @@
 
 def kernel(
     count, slot_rows, slot_cols, tiles_hbm, elec_dev, phon_dev, elec_source, phon_source, elec_rate, phon_rate,
-    elec_out, phon_out,
+    sums,
     tiles, seg_p, seg_e, pb_0, pb_1, pb_2, eb_0, eb_1, eb_2, psend, precv, dsend, drecv, esend, erecv, kept, tmp,
     whole_v, parts_v, whole, parts, load_sems, table_sems, send_sems, recv_sems,
 ):
@@ -394,7 +394,7 @@
             if s < ITERS:
                 pb[s][3 * el + i, rows, :] = (total / phon_rate[i]).astype(jnp.bfloat16)
             else:
-                phon_out[i, rows, :] = total
+                sums[1 + i, rows, :] = total
             return carry
 
         over(3, 0, own_p(el, h), [mail[m][4] for m in needs], visit)
@@ -410,7 +410,7 @@
             if s < ITERS:
                 eb[s][ph, rows, :] = (total / elec_rate[...]).astype(jnp.bfloat16)
             else:
-                elec_out[rows, :] = total
+                sums[0, rows, :] = total
             return carry
 
         over(2, 0, kept_e(0), [mail[m][4] for m in needs], visit)
@@ -456,20 +456,23 @@
         left(key)
 
 
+def finish(sums, elec_rate, phon_rate, elec_out, phon_out):
+    elec_out[...] = sums[0] / elec_rate[...]
+    for block in range(phon_out.shape[0]):
+        phon_out[block] = sums[1 + block] / phon_rate[block]
+
+
 def local(
     elec_dev, phon_dev, elec_source, phon_source, elec_rate, phon_rate, tiles, tile_rows, tile_cols, tile_count
 ):
     slots, side, _ = tiles.shape[2:]
     rhs = elec_dev.shape[1]
     vmem, smem = pl.BlockSpec(memory_space=pltpu.VMEM), pl.BlockSpec(memory_space=pltpu.SMEM)
-    elec_sum, phon_sum = pl.pallas_call(
+    sums = pl.pallas_call(
         kernel,
-        out_shape=(
-            jax.ShapeDtypeStruct((rhs, side), jnp.float32),
-            jax.ShapeDtypeStruct((3, rhs, side), jnp.float32),
-        ),
+        out_shape=jax.ShapeDtypeStruct((4, rhs, side), jnp.float32),
         in_specs=[smem, vmem, vmem, pl.BlockSpec(memory_space=pl.ANY)] + [vmem] * 6,
-        out_specs=(vmem, vmem),
+        out_specs=vmem,
         scratch_shapes=[
             pltpu.VMEM((slots, side, side), jnp.bfloat16),
             pltpu.VMEM((slots, rhs, side), jnp.float32),
@@ -509,7 +512,18 @@
         elec_rate,
         phon_rate[0][:, None, :],
     )
-    return elec_sum[None] / elec_rate[:, None, :], phon_sum[None] / phon_rate[:, :, None, :]
+    elec_out, phon_out = pl.pallas_call(
+        finish,
+        out_shape=(
+            jax.ShapeDtypeStruct((rhs, side), jnp.float32),
+            jax.ShapeDtypeStruct((3, rhs, side), jnp.float32),
+        ),
+        in_specs=[vmem] * 3,
+        out_specs=(vmem, vmem),
+        compiler_params=pltpu.CompilerParams(vmem_limit_bytes=8 * 2**20),
+        name="finish",
+    )(sums, elec_rate, phon_rate[0][:, None, :])
+    return elec_out[None], phon_out[None]
 
 
 def solution(mesh):

time: 120 us -> 117 us (0.975)
  other arithmetic: 3.25 us -> 0 us
    div x2 -> x0, other arithmetic: 3.25 us -> none  [the longest x1 1.7 us: local(): phon_sum[None] / phon_rate[:, :, None, :]]
    pallas_call x1 -> x2, Pallas kernels: 115 us -> 114 us  [the longest x1 114 us: local(): pl.pallas_call(kernel, out_shape=jax.ShapeDtypeStruct((4, rhs, side), jnp...]
where the time goes in v4:
time: 117 us
  Pallas kernels  114 us (97%)
  between operations  1.35 us (1%)
    pallas_call x1, Pallas kernels, local(): pl.pallas_call(kernel, out_shape=jax.ShapeDtypeStruct((4, rhs, side), jnp...  114 us

profile of v4, /device:TPU:0, one launch (start us, length us, event | category | flops | bytes accessed | tf_op | source)
XLA Modules:
  0.0 116.8 jit_solution(9217600185352041631)
XLA Ops:
  0.6 0.0 copy-start.2
  0.6 0.0 copy-start.1
  1.3 113.7 %sweeps.1.sums = f32[4,96,256]{2,1,0:T(8,128)} custom-call(s32[1,1]{1,0:T(1,128)S(6)} %copy.12.count, s32[1,128]{1,0:T(1,128)} %bitcast.17, s32[1,128]{1,0:T(1,128)} %bitcast.18, bf16[128,256,256]{2,1,0:T(8,128)(2,1)} %bitcast.12, f32[96,256]{1,0:T(8,128)} %bitcast.15, f32[3,96,256]{2,1,0:T(8,128)} %bitcast.13, f32[96,256]{1,0:T(8,128)} %bitcast.16, ...), custom_call_target="tpu_custom_call" | custom-call | tf_op jit(solution)/shard_map/sweeps/pallas_call | solution.py:471
  115.0 0.0 copy-done.2
  115.0 0.0 copy-done.1
  115.0 0.0 copy-start
  115.1 1.0 copy-done
  116.0 0.8 finish.1
Async XLA Ops:
  0.6 114.4 %copy-start.2 = (f32[1,256]{1,0:T(1,128)S(1)}, f32[1,256]{1,0:T(1,128)}, u32[]{:S(2)}) copy-start(f32[1,256]{1,0:T(1,128)} %elec_rate.3) | copy-start | bytes 3076
  0.6 114.4 %copy-start.1 = (f32[1,3,256]{2,0,1:T(1,128)S(1)}, f32[1,3,256]{2,0,1:T(1,128)}, u32[]{:S(2)}) copy-start(f32[1,3,256]{2,0,1:T(1,128)} %param.15) | copy-start | bytes 9220
  115.0 1.0 copy-start
